TPU v7x, 32 devices: a whole 2x2x4 slice. The times are simulated.
32 devices in a mesh: dp: 4 (over z), expert: 8 (over y, x, core).
Axes of the slice: x: 2, y: 2, z: 4, core: 2. Of those that a mesh axis runs over, the one named last changes fastest.
Arguments:
- hidden: bfloat16 [4, 1024, 2048], P('dp', 'expert'), may hold values from -6 to 6
- output_cotangent: bfloat16 [4, 1024, 2048], P('dp', 'expert'), may hold values from -6 to 6
- attention_gain: float32 [2048], replicated, may hold values from 0.5 to 1.5
- expert_norm_gain: float32 [2048], replicated, may hold values from 0.5 to 1.5
- query_key_value_weight: bfloat16 [3, 2048, 2048], P(None, None, 'expert'), may hold values from -0.125 to 0.125
- output_weight: bfloat16 [2048, 2048], P('expert'), may hold values from -0.5 to 0.5
- gate_up_weight: bfloat16 [16, 2, 2048, 1024], P('expert'), may hold values from -0.125 to 0.125
- down_weight: bfloat16 [16, 1024, 2048], P('expert'), may hold values from -0.1875 to 0.1875
- token_experts: int32 [4, 1024, 8], P('dp', 'expert'), may hold values from 0 to 15, all different within a row; in each aligned block of 128 rows (0 to 127, 128 to 255, ..., all dimensions but the last counted through in order) at most 80 rows name the same one
- expert_gate_weight: float32 [4, 1024, 8], P('dp', 'expert'), may hold values from 0.05 to 0.25
- sequence_adapter: int32 [4], replicated, may hold values from 0 to 7
- optimizer_steps: int32 [1], replicated, may hold values from 1 to 20
- adapter_attention_input: bfloat16 [3, 8, 16, 2048], replicated, may hold values from -0.125 to 0.125
- adapter_attention_output: bfloat16 [3, 8, 16, 2048], P(None, None, None, 'expert'), may hold values from -0.375 to 0.375
- adapter_projection_input: bfloat16 [8, 16, 2048], P(None, None, 'expert'), may hold values from -0.5 to 0.5
- adapter_projection_output: bfloat16 [8, 16, 2048], replicated, may hold values from -0.375 to 0.375
- adapter_hidden_input: bfloat16 [16, 2, 8, 16, 2048], P('expert'), may hold values from -0.125 to 0.125
- adapter_hidden_output: bfloat16 [16, 2, 8, 16, 1024], P('expert'), may hold values from -0.375 to 0.375
- adapter_down_input: bfloat16 [16, 8, 16, 1024], P('expert'), may hold values from -0.1875 to 0.1875
- adapter_down_output: bfloat16 [16, 8, 16, 2048], P('expert'), may hold values from -0.375 to 0.375
- moment_attention_input: float32 [3, 8, 16, 2048], P(None, None, None, ('dp', 'expert')), may hold values from -0.036 to 0.036
- moment_attention_output: float32 [3, 8, 16, 2048], P(None, None, None, ('expert', 'dp')), may hold values from -0.036 to 0.036
- moment_projection_input: float32 [8, 16, 2048], P(None, None, ('expert', 'dp')), may hold values from -0.036 to 0.036
- moment_projection_output: float32 [8, 16, 2048], P(None, None, ('dp', 'expert')), may hold values from -0.036 to 0.036
- moment_hidden_input: float32 [16, 2, 8, 16, 2048], P('expert', None, None, None, 'dp'), may hold values from -0.036 to 0.036
- moment_hidden_output: float32 [16, 2, 8, 16, 1024], P('expert', None, None, None, 'dp'), may hold values from -0.036 to 0.036
- moment_down_input: float32 [16, 8, 16, 1024], P('expert', None, None, 'dp'), may hold values from -0.036 to 0.036
- moment_down_output: float32 [16, 8, 16, 2048], P('expert', None, None, 'dp'), may hold values from -0.036 to 0.036
- squared_attention_input: float32 [3, 8, 16, 2048], P(None, None, None, ('dp', 'expert')), may hold values from 2e-05 to 0.001
- squared_attention_output: float32 [3, 8, 16, 2048], P(None, None, None, ('expert', 'dp')), may hold values from 2e-05 to 0.001
- squared_projection_input: float32 [8, 16, 2048], P(None, None, ('expert', 'dp')), may hold values from 2e-05 to 0.001
- squared_projection_output: float32 [8, 16, 2048], P(None, None, ('dp', 'expert')), may hold values from 2e-05 to 0.001
- squared_hidden_input: float32 [16, 2, 8, 16, 2048], P('expert', None, None, None, 'dp'), may hold values from 2e-05 to 0.001
- squared_hidden_output: float32 [16, 2, 8, 16, 1024], P('expert', None, None, None, 'dp'), may hold values from 2e-05 to 0.001
- squared_down_input: float32 [16, 8, 16, 1024], P('expert', None, None, 'dp'), may hold values from 2e-05 to 0.001
- squared_down_output: float32 [16, 8, 16, 2048], P('expert', None, None, 'dp'), may hold values from 2e-05 to 0.001
Outputs:
- block_out: bfloat16 [4, 1024, 2048], P('dp', 'expert')
- grad_hidden: float32 [4, 1024, 2048], P('dp', 'expert')
- global_norm: float32 [1], replicated
- grad_qkv_a: float32 [3, 8, 16, 2048], P(None, None, None, ('dp', 'expert'))
- new_first_qkv_a: float32 [3, 8, 16, 2048], P(None, None, None, ('dp', 'expert'))
- new_second_qkv_a: float32 [3, 8, 16, 2048], P(None, None, None, ('dp', 'expert'))
- update_qkv_a: float32 [3, 8, 16, 2048], P(None, None, None, ('dp', 'expert'))
- grad_qkv_b: float32 [3, 8, 16, 2048], P(None, None, None, ('expert', 'dp'))
- new_first_qkv_b: float32 [3, 8, 16, 2048], P(None, None, None, ('expert', 'dp'))
- new_second_qkv_b: float32 [3, 8, 16, 2048], P(None, None, None, ('expert', 'dp'))
- update_qkv_b: float32 [3, 8, 16, 2048], P(None, None, None, ('expert', 'dp'))
- grad_out_a: float32 [8, 16, 2048], P(None, None, ('expert', 'dp'))
- new_first_out_a: float32 [8, 16, 2048], P(None, None, ('expert', 'dp'))
- new_second_out_a: float32 [8, 16, 2048], P(None, None, ('expert', 'dp'))
- update_out_a: float32 [8, 16, 2048], P(None, None, ('expert', 'dp'))
- grad_out_b: float32 [8, 16, 2048], P(None, None, ('dp', 'expert'))
- new_first_out_b: float32 [8, 16, 2048], P(None, None, ('dp', 'expert'))
- new_second_out_b: float32 [8, 16, 2048], P(None, None, ('dp', 'expert'))
- update_out_b: float32 [8, 16, 2048], P(None, None, ('dp', 'expert'))
- grad_in_a: float32 [16, 2, 8, 16, 2048], P('expert', None, None, None, 'dp')
- new_first_in_a: float32 [16, 2, 8, 16, 2048], P('expert', None, None, None, 'dp')
- new_second_in_a: float32 [16, 2, 8, 16, 2048], P('expert', None, None, None, 'dp')
- update_in_a: float32 [16, 2, 8, 16, 2048], P('expert', None, None, None, 'dp')
- grad_mid_b: float32 [16, 2, 8, 16, 1024], P('expert', None, None, None, 'dp')
- new_first_mid_b: float32 [16, 2, 8, 16, 1024], P('expert', None, None, None, 'dp')
- new_second_mid_b: float32 [16, 2, 8, 16, 1024], P('expert', None, None, None, 'dp')
- update_mid_b: float32 [16, 2, 8, 16, 1024], P('expert', None, None, None, 'dp')
- grad_down_a: float32 [16, 8, 16, 1024], P('expert', None, None, 'dp')
- new_first_down_a: float32 [16, 8, 16, 1024], P('expert', None, None, 'dp')
- new_second_down_a: float32 [16, 8, 16, 1024], P('expert', None, None, 'dp')
- update_down_a: float32 [16, 8, 16, 1024], P('expert', None, None, 'dp')
- grad_down_b: float32 [16, 8, 16, 2048], P('expert', None, None, 'dp')
- new_first_down_b: float32 [16, 8, 16, 2048], P('expert', None, None, 'dp')
- new_second_down_b: float32 [16, 8, 16, 2048], P('expert', None, None, 'dp')
- update_down_b: float32 [16, 8, 16, 2048], P('expert', None, None, 'dp')
Inputs may be any that keep to these rules, and one draw needn't show every extreme that they name: `token_experts`: in each aligned block of 128 positions (the rows of one device) no expert is named by more than 80 assignments; this bound is reached in some block.
All inputs are finite; a program needn't handle non-finite values.
Results may differ from a plain program's by a relative error of at most 0.02.
Values may be sent and summed in bfloat16 or wider, within the bound.
A program may use at most 256 MiB of HBM per device.

v0:
```python
import functools

import jax
import jax.numpy as jnp
from jax import lax
from jax.experimental import pallas as pl
from jax.experimental.pallas import tpu as pltpu
from jax.sharding import PartitionSpec as P


single = jnp.float32
brain = jnp.bfloat16
HEAD = 128
TILE = 256
CHUNKS = 4
ORDER = [k + j * (CHUNKS // 2) for k in range(CHUNKS // 2) for j in range(2)]
GATHER_SENDS = CHUNKS * 7
SCATTER_SEMS = CHUNKS * 7
norm_eps = 1e-05
VMEM_ALL = 67043328


def dot(a, b, left=1, right=0):
    return lax.dot_general(a, b, (((left,), (right,)), ((), ())), preferred_element_type=single)


def peers():
    me = lax.axis_index("expert")
    core = me + 1 - 2 * (me % 2)
    across = me + 2 - 4 * ((me // 2) % 2)
    along = me + 4 - 8 * (me // 4)
    return me, core, across, along


def greet():
    me, core, across, along = peers()
    barrier = pltpu.get_barrier_semaphore()
    for peer in (core, across, along):
        pl.semaphore_signal(barrier, inc=1, device_id={"expert": peer})
    pl.semaphore_wait(barrier, 3)


class Mover:
    def __init__(self, send_sem, recv_sem):
        self.send_sem, self.recv_sem = send_sem, recv_sem
        self.me, self.core, self.across, self.along = peers()
        self.far = self.across + self.along - self.me
        self.count = 0
        self.waiting = []

    def go(self, src, dst, recv, peer):
        pltpu.make_async_remote_copy(
            src_ref=src, dst_ref=dst, send_sem=self.send_sem.at[self.count],
            recv_sem=self.recv_sem.at[recv], device_id={"expert": peer},
        ).start()
        self.count += 1

    def later(self, args):
        self.waiting.append(args)
        if len(self.waiting) > 1:
            self.waiting.pop(0)()

    def flush(self):
        while self.waiting:
            self.waiting.pop(0)()

    def got(self, view, recv):
        pltpu.make_async_remote_copy(
            src_ref=view, dst_ref=view, send_sem=self.send_sem.at[0], recv_sem=self.recv_sem.at[recv],
            device_id={"expert": self.core},
        ).wait_recv()

    def drain(self):
        view = self.sample()
        for i in range(self.count):
            pltpu.make_async_remote_copy(
                src_ref=view, dst_ref=view, send_sem=self.send_sem.at[i], recv_sem=self.recv_sem.at[0],
                device_id={"expert": self.core},
            ).wait_send()

    def beside(self, block):
        return block + 1 - 2 * (self.me % 2)


class Gather(Mover):
    def __init__(self, out, send_sem, recv_sem):
        super().__init__(send_sem, recv_sem)
        self.out = out
        self.size = out.shape[1] // CHUNKS

    def sample(self):
        return self.out.at[0, pl.ds(0, self.size)]

    def move(self, block, k, peer):
        view = self.out.at[block, pl.ds(k * self.size, self.size)]
        self.go(view, view, block * CHUNKS + k, peer)

    def arrive(self, block, k):
        self.got(self.out.at[block, pl.ds(k * self.size, self.size)], block * CHUNKS + k)

    def start_own(self, k):
        for peer in (self.across, self.along, self.core):
            self.move(self.me, k, peer)

    def start(self):
        for k in ORDER:
            self.start_own(k)

    def relay(self, i):
        k = ORDER[i]
        first_half = k < CHUNKS // 2
        self.arrive(self.across, k)
        if first_half:
            self.move(self.across, k, self.along)
        self.move(self.across, k, self.core)
        self.arrive(self.along, k)
        if not first_half:
            self.move(self.along, k, self.across)
        self.move(self.along, k, self.core)

    def relay_far(self, i):
        half = CHUNKS // 2
        for k in (i, i + half):
            self.arrive(self.far, k)
            self.move(self.far, k, self.core)

    def pair(self, block):
        for k in range(CHUNKS):
            self.arrive(self.beside(block), k)


class Scatter(Mover):
    def __init__(self, part, pair, half_x, half_y, from_x, from_y, send_sem, recv_sem, own=None):
        super().__init__(send_sem, recv_sem)
        self.part, self.pair, self.own = part, pair, own
        self.half_x, self.half_y, self.from_x, self.from_y = half_x, half_y, from_x, from_y
        self.order = (self.far, self.across, self.along, self.me)
        self.toks = pair.shape[1]
        self.size = self.toks // CHUNKS
        half = CHUNKS // 2
        self.hx = 4 * CHUNKS
        self.hy = self.hx + half
        self.fx = self.hy + half
        self.fy = self.fx + CHUNKS

    def sample(self):
        return self.pair.at[0, self.rows(0)]

    def rows(self, k):
        return pl.ds(k * self.size, self.size)

    def chunk(self, block, k):
        if len(self.part.shape) == 3:
            return self.part.at[block, self.rows(k)]
        return self.part.at[pl.ds(pl.multiple_of(block * self.toks + k * self.size, self.size), self.size)]

    def mine(self, i, k):
        view = self.chunk(self.order[i], k) if self.own is None else self.own.at[i, self.rows(k)]
        return view[...].astype(single)

    def give(self, i):
        other = self.beside(self.order[i])
        for k in range(CHUNKS):
            r = self.rows(k)
            self.go(self.chunk(other, k), self.pair.at[i, r], i * CHUNKS + k, self.core)

    def add(self, i, k, extra=None):
        r = self.rows(k)
        self.got(self.pair.at[i, r], i * CHUNKS + k)
        total = self.mine(i, k) + self.pair[i, r].astype(single)
        if extra is not None:
            ref, recv, k2 = extra
            r2 = self.rows(k2)
            self.got(ref.at[r2], recv)
            total = total + ref[r2].astype(single)
        self.pair[i, r] = total.astype(brain)

    def steps(self):
        half = CHUNKS // 2
        out = []

        def relay(i, k, to, row, recv, peer):
            self.later(lambda: self.go(self.pair.at[i, self.rows(k)], to.at[self.rows(row)], recv, peer))

        def one(k):
            self.add(0, k)
            relay(0, k, self.half_x, k, self.hx + k, self.across)
            self.add(0, k + half)
            relay(0, k + half, self.half_y, k, self.hy + k, self.along)

        def two(k):
            self.add(1, k)
            relay(1, k, self.from_x, k, self.fx + k, self.across)
            self.add(2, k + half)
            relay(2, k + half, self.from_y, k + half, self.fy + k + half, self.along)

        def three(k):
            self.add(1, k + half, (self.half_y, self.hy + k, k))
            relay(1, k + half, self.from_x, k + half, self.fx + k + half, self.across)
            self.add(2, k, (self.half_x, self.hx + k, k))
            relay(2, k, self.from_y, k, self.fy + k, self.along)

        for fn in (one, two, three):
            for k in range(half):
                out.append(functools.partial(fn, k))
        out.append(self.flush)
        return out

    def final(self, k):
        r = self.rows(k)
        self.got(self.pair.at[3, r], 3 * CHUNKS + k)
        total = self.mine(3, k) + self.pair[3, r].astype(single)
        self.got(self.from_x.at[r], self.fx + k)
        total = total + self.from_x[r].astype(single)
        self.got(self.from_y.at[r], self.fy + k)
        return total + self.from_y[r].astype(single)


def scatter_scratch(rows, cols):
    return [
        pltpu.VMEM((4, rows, cols), brain),
        pltpu.VMEM((rows // 2, cols), brain),
        pltpu.VMEM((rows // 2, cols), brain),
        pltpu.VMEM((rows, cols), brain),
        pltpu.VMEM((rows, cols), brain),
        pltpu.SemaphoreType.DMA((SCATTER_SEMS,)),
        pltpu.SemaphoreType.DMA((SCATTER_SEMS,)),
    ]


def gather_scratch(n):
    return [pltpu.SemaphoreType.DMA((GATHER_SENDS,)), pltpu.SemaphoreType.DMA((n * CHUNKS,))]


def rms(values, gain):
    return values * lax.rsqrt(jnp.mean(values * values, axis=-1, keepdims=True) + norm_eps) * gain


def fetch(src, dst, sem):
    copy = pltpu.make_async_copy(src, dst, sem)
    copy.start()
    return copy


def drive(count, body, events):
    def step(i, carry):
        body(i)
        for at, actions in events.items():

            @pl.when(i == at)
            def _(actions=actions):
                for action in actions:
                    action()

        return carry

    lax.fori_loop(0, count, step, 0)


def slots_of(denseall_ref, me, experts, dense, place):
    blocks, toks = denseall_ref.shape[0], denseall_ref.shape[2]
    for b in range(blocks):
        for e in range(experts):
            at = experts * b + e
            dense[at : at + 1, :] = denseall_ref[b, pl.ds(experts * me + e, 1), :]
    upper = (
        lax.broadcasted_iota(jnp.int32, (toks, toks), 0) < lax.broadcasted_iota(jnp.int32, (toks, toks), 1)
    ).astype(single).astype(brain)
    chosen = dense[...] > 0.0
    before = dot(chosen.astype(single).astype(brain), upper)
    place[...] = jnp.where(chosen, before, -1.0)


def picks(place, b, cap, experts):
    rows = lax.broadcasted_iota(jnp.int32, (cap, place.shape[1]), 0).astype(single)
    return [(place[pl.ds(experts * b + e, 1), :] == rows).astype(single) for e in range(experts)]


def weigh(place, dense, weight, b, cap, experts):
    for e, sel in enumerate(picks(place, b, cap, experts)):
        w = jnp.sum(sel * dense[pl.ds(experts * b + e, 1), :], axis=1, keepdims=True)
        weight[e, pl.ds(pl.multiple_of(b * cap, 16), cap), :] = w


def take(place, block, rows, b, cap):
    experts = rows.shape[0]
    both = jnp.concatenate([s.astype(brain) for s in picks(place, b, cap, experts)], axis=0)
    got = dot(both, block).astype(brain)
    at = pl.ds(pl.multiple_of(b * cap, 16), cap)
    for e in range(experts):
        rows[e, at, :] = got[e * cap : (e + 1) * cap]


def combined(place, rows, b, cap, apart):
    experts = rows.shape[0] // apart
    both = jnp.concatenate([s.astype(brain) for s in picks(place, b, cap, experts)], axis=0)
    parts = [rows[pl.ds(pl.multiple_of(e * apart + b * cap, 16), cap), :] for e in range(experts)]
    return dot(both, jnp.concatenate(parts, axis=0), 0, 0).astype(brain)


def two(p, toks):
    return pl.ds(pl.multiple_of(p * 2 * toks, 2 * toks), 2 * toks)


def meet(n, replicas, with_dp):
    me, rep = lax.axis_index("expert"), lax.axis_index("dp")
    barrier = pltpu.get_barrier_semaphore()
    for j in range(1, n):
        pl.semaphore_signal(barrier, inc=1, device_id={"expert": (me + j) % n})
    if with_dp:
        for j in range(1, replicas):
            pl.semaphore_signal(barrier, inc=1, device_id={"dp": (rep + j) % replicas})
    pl.semaphore_wait(barrier, n - 1 + (replicas - 1 if with_dp else 0))


def front_kernel(
    cap, ids_ref, hid_ref, top_ref, routes_ref, gates_ref, gain_ref, gain2_ref,
    w_hbm, a_hbm, b_hbm, wo_hbm, pa_hbm, pb_hbm, dn_hbm, da_hbm, db_hbm,
    low_ref, lse_ref, denseall_ref, orank_ref, gdr_ref, seq_hbm, proj_hbm, mixed_hbm, resid_hbm, x_hbm, g_hbm, ga_hbm,
    part, seq_ref, proj_ref, mixed_ref, topseq_ref, resid_ref, moe_ref, x_rows, g_rows, ga,
    w_ref, a_all, b_all, wo_ref, pa_all, pb_all, dn, da_all, db_all, a_ref, b_ref, mydense, dense, place, weight,
    load_sem, save_sem, *sems,
):
    toks, width = hid_ref.shape
    span = w_ref.shape[2]
    heads = span // HEAD
    n = seq_ref.shape[0]
    length = toks * n
    experts, hidden = dn.shape[0], dn.shape[1]
    loads = [
        fetch(src, dst, load_sem.at[i])
        for i, (src, dst) in enumerate(
            (
                (w_hbm, w_ref), (a_hbm, a_all), (b_hbm, b_all), (pa_hbm, pa_all), (pb_hbm, pb_all), (wo_hbm, wo_ref),
                (da_hbm, da_all), (db_hbm, db_all), (dn_hbm, dn),
            )
        )
    ]
    seq_g = Gather(seq_ref, sems[0], sems[1])
    top_g = Gather(topseq_ref, sems[2], sems[3])
    moe_g = Gather(moe_ref, sems[4], sems[5])
    red = Scatter(part, *sems[6:13])
    dsend, drecv = sems[13:15]
    me = seq_g.me
    slot = ids_ref[lax.axis_index("dp")]
    saves = []

    def save(src, dst):
        saves.append(fetch(src, dst, save_sem.at[len(saves)]))

    seq_ref[me] = rms(hid_ref[...].astype(single), gain_ref[...]).astype(brain)
    topseq_ref[me] = top_ref[...]
    choices = lax.broadcasted_iota(jnp.int32, (mydense.shape[0], toks), 0)
    table = jnp.zeros(mydense.shape, single)
    for k in range(routes_ref.shape[0]):
        table = table + jnp.where(routes_ref[k : k + 1, :] == choices, gates_ref[k : k + 1, :], 0.0)
    mydense[...] = table
    denseall_ref[me] = table
    meet(n, 1, False)
    seq_g.start()

    def dense_copy(j):
        return pltpu.make_async_remote_copy(
            src_ref=mydense, dst_ref=denseall_ref.at[me], send_sem=dsend.at[j - 1], recv_sem=drecv.at[me],
            device_id={"expert": (me + j) % n},
        )

    for j in range(1, n):
        dense_copy(j).start()
    for copy in loads[:3]:
        copy.wait()
    b_ref[...] = jnp.zeros_like(b_ref)
    for j in range(3):
        a_ref[16 * j : 16 * j + 16, :] = a_all[j, slot]
        b_ref[j, 16 * j : 16 * j + 16, :] = b_all[j, slot]

    def qkv(block):
        p = block // 2
        at = two(p, toks)
        low_ref[at, :] = dot(seq_ref[pl.ds(2 * p, 2)].reshape(2 * toks, width), a_ref[...], 1, 1).astype(brain)

        def third(j, carry):
            both = seq_ref[pl.ds(2 * p, 2)].reshape(2 * toks, width)
            proj_ref[j, at, :] = (dot(both, w_ref[j]) + dot(low_ref[at, :], b_ref[j])).astype(brain)
            return carry

        lax.fori_loop(0, 3, third, 0)

    seq_g.pair(me)
    qkv(me)
    for i in range(CHUNKS):
        seq_g.relay(i)
    top_g.start()
    seq_g.pair(seq_g.across)
    qkv(seq_g.across)
    for i in range(CHUNKS // 2):
        seq_g.relay_far(i)
    seq_g.pair(seq_g.along)
    qkv(seq_g.along)
    seq_g.pair(seq_g.far)
    qkv(seq_g.far)
    save(seq_ref, seq_hbm)
    save(proj_ref, proj_hbm)

    scale = HEAD ** (-0.5)
    block = 256
    top_steps = [functools.partial(top_g.relay, i) for i in range(CHUNKS)]
    top_steps += [functools.partial(top_g.relay_far, i) for i in range(CHUNKS // 2)]

    for h in range(heads):
        at = slice(h * HEAD, (h + 1) * HEAD)

        def attend(i, h=h, at=at):
            r = pl.ds(pl.multiple_of(i * block, block), block)
            scores = dot(proj_ref[0, r, at], proj_ref[1, :, at], 1, 1) * scale
            peak = jnp.max(scores, axis=-1, keepdims=True)
            expo = jnp.exp(scores - peak)
            total = jnp.sum(expo, axis=-1, keepdims=True)
            probs = (expo * (1.0 / total)).astype(brain)
            mixed_ref[r, at] = dot(probs, proj_ref[2, :, at]).astype(brain)
            lse_ref[r, h : h + 1] = peak + jnp.log(total)

        drive(length // block, attend, {1: top_steps[3 * h : 3 * h + 1], 3: top_steps[3 * h + 1 : 3 * h + 3]})
    del top_steps[: 3 * heads]
    for copy in loads[3:6]:
        copy.wait()

    for i in range(4):
        p = red.order[i] // 2
        at = two(p, toks)
        rank = dot(mixed_ref[at, :], pa_all[slot], 1, 1).astype(brain)
        orank_ref[at, :] = rank
        cols = min(1024, width)

        def project(c, carry, p=p, at=at):
            s = pl.ds(pl.multiple_of(c * cols, cols), cols)
            out = dot(mixed_ref[at, :], wo_ref[:, s]) + dot(orank_ref[at, :], pb_all[slot, :, s])
            part[pl.ds(2 * p, 2), :, s] = out.astype(brain).reshape(2, toks, cols)
            return carry

        lax.fori_loop(0, width // cols, project, 0)
        if i:
            red.give(i - 1)
    red.give(3)
    save(mixed_ref, mixed_hbm)
    for step in top_steps:
        step()
    for block_at in (me, top_g.across, top_g.along, top_g.far):
        top_g.pair(block_at)
    for j in range(1, n):
        src = (me + j) % n
        view = denseall_ref.at[src]
        pltpu.make_async_remote_copy(
            src_ref=view, dst_ref=view, send_sem=dsend.at[0], recv_sem=drecv.at[src], device_id={"expert": src}
        ).wait_recv()
    for j in range(1, n):
        dense_copy(j).wait_send()
    slots_of(denseall_ref, me, experts, dense, place)
    steps = red.steps()

    def top_rows(b):
        weigh(place, dense, weight, b, cap, experts)
        take(place, topseq_ref[b], g_rows, b, cap)

    drive(n, top_rows, {1: steps[0:1], 2: steps[1:2], 3: steps[2:3], 4: steps[3:4]})
    for copy in loads[6:]:
        copy.wait()

    def top_rank(e):
        gdr_ref[e] = (dot(g_rows[e], db_all[e, slot], 1, 1) * weight[e]).astype(brain)

    drive(experts, top_rank, {})
    half = n * cap // 2
    tiles = hidden // TILE

    def top_tile(t):
        e, f, m = t // (2 * tiles), t // 2 % tiles, t % 2
        at = pl.ds(pl.multiple_of(f * TILE, TILE), TILE)
        r = pl.ds(pl.multiple_of(m * half, 16), half)
        out = dot(g_rows[e, r, :], dn[e, at, :], 1, 1) * weight[e, r, :]
        ga[e, r, at] = (out + dot(gdr_ref[e, r, :], da_all[e, slot, :, at])).astype(brain)

    drive(2 * experts * tiles, top_tile, {2: steps[4:5], 4: steps[5:6], 5: steps[6:7]})
    save(g_rows, g_hbm)
    save(ga, ga_hbm)
    for k in ORDER:
        r = red.rows(k)
        resid = hid_ref[r].astype(single) + red.final(k)
        resid_ref[r] = resid
        moe_ref[me, r] = rms(resid, gain2_ref[...]).astype(brain)
        if k != ORDER[0]:
            moe_g.start_own(ORDER[ORDER.index(k) - 1])
    save(resid_ref, resid_hbm)
    moe_g.start_own(ORDER[-1])

    def moe_rows(block_at):
        p = block_at // 2

        def one(i, carry):
            take(place, moe_ref[2 * p + i], x_rows, 2 * p + i, cap)
            return carry

        lax.fori_loop(0, 2, one, 0)

    moe_g.pair(me)
    moe_rows(me)
    for i in range(CHUNKS):
        moe_g.relay(i)
    moe_g.pair(moe_g.across)
    moe_rows(moe_g.across)
    for i in range(CHUNKS // 2):
        moe_g.relay_far(i)
    moe_g.pair(moe_g.along)
    moe_rows(moe_g.along)
    moe_g.pair(moe_g.far)
    moe_rows(moe_g.far)
    save(x_rows, x_hbm)
    for mover in (seq_g, top_g, red, moe_g):
        mover.drain()
    for copy in saves:
        copy.wait()


def front(ids, hid, top, routes, gates, gain, gain2, w, a, b, wo, pa, pb, dn, da, db, n, cap, cid=0):
    toks, width = hid.shape
    span = w.shape[2]
    length = toks * n
    experts, hidden = dn.shape[0], dn.shape[1]
    rows = n * cap
    vm = pl.BlockSpec(memory_space=pltpu.VMEM)
    sm = pl.BlockSpec(memory_space=pltpu.SMEM)
    hb = pl.BlockSpec(memory_space=pl.ANY)
    f = lambda *s: jax.ShapeDtypeStruct(s, single)
    h = lambda *s: jax.ShapeDtypeStruct(s, brain)
    bv = lambda *s: pltpu.VMEM(s, brain)
    fv = lambda *s: pltpu.VMEM(s, single)
    whole = bv(n, toks, width)
    return pl.pallas_call(
        functools.partial(front_kernel, cap),
        out_shape=(
            h(length, 48), f(length, span // HEAD), f(n, experts * n, toks), h(length, 16), h(experts, rows, 16),
            h(n, toks, width), h(3, length, span), h(length, span), f(toks, width),
            h(experts, rows, width), h(experts, rows, width), h(experts, rows, hidden),
        ),
        in_specs=[sm] + [vm] * 6 + [hb] * 9,
        out_specs=[vm] * 5 + [hb] * 7,
        scratch_shapes=[
            whole, whole, bv(3, length, span), bv(length, span), whole, fv(toks, width), whole,
            bv(experts, rows, width), bv(experts, rows, width), bv(experts, rows, hidden),
        ]
        + [pltpu.VMEM(v.shape, brain) for v in (w, a, b, wo, pa, pb, dn, da, db)]
        + [
            bv(48, width), bv(3, 48, span), fv(experts * n, toks), fv(n * experts, toks), fv(n * experts, toks),
            fv(experts, rows, 1), pltpu.SemaphoreType.DMA((9,)), pltpu.SemaphoreType.DMA((7,)),
        ]
        + gather_scratch(n) + gather_scratch(n) + gather_scratch(n) + scatter_scratch(toks, width)
        + [pltpu.SemaphoreType.DMA((n,)), pltpu.SemaphoreType.DMA((n,))],
        compiler_params=pltpu.CompilerParams(collective_id=cid, has_side_effects=True, vmem_limit_bytes=VMEM_ALL),
        name="front",
    )(ids, hid, top, routes, gates, gain, gain2, w, a, b, wo, pa, pb, dn, da, db)


def moe_kernel(
    cap, replicas, ids_ref, denseall_ref, gdr_ref, x_hbm, g_hbm, ga_hbm, gu_hbm, ha_hbm, hb_hbm, da_hbm,
    drank_ref, gina_ref, gmidb_ref, gdna_ref, gdnb_ref, gpart_hbm, act_hbm,
    gu, x_rows, g_rows, ga, s_rows, act, gg, uu, dense, place, weight, irank, girank, ha_ref, hb_ref, da_ref,
    out_stage, pick_sem, x_sem, g_sem, ga_sem, gu_sem, act_sem, out_sem,
):
    experts, width, hidden = gu.shape[0], gu.shape[2], gu.shape[3]
    blocks = denseall_ref.shape[0]
    rows = x_rows.shape[1]
    tiles = hidden // TILE
    me = lax.axis_index("expert")
    which = ids_ref[lax.axis_index("dp")]
    picked = []
    for e in range(experts):
        for i in range(2):
            picked.append((ha_hbm.at[e, i, which], ha_ref.at[e, pl.ds(16 * i, 16)]))
            picked.append((hb_hbm.at[e, i, which], hb_ref.at[e, i]))
        picked.append((da_hbm.at[e, which], da_ref.at[e]))

    def cols(f):
        return pl.ds(pl.multiple_of(f * TILE, TILE), TILE)

    x_copy = lambda e: pltpu.make_async_copy(x_hbm.at[e], x_rows.at[e], x_sem.at[e])
    g_copy = lambda e: pltpu.make_async_copy(g_hbm.at[e], g_rows.at[e], g_sem.at[e])
    ga_copy = lambda e: pltpu.make_async_copy(ga_hbm.at[e], ga.at[e], ga_sem.at[e])
    gu_copy = lambda e, f: pltpu.make_async_copy(
        gu_hbm.at[e, :, :, cols(f)], gu.at[e, :, :, cols(f)], gu_sem.at[e, f]
    )
    act_copy = lambda e: pltpu.make_async_copy(act.at[e], act_hbm.at[e], act_sem.at[e])
    x_copy(0).start()
    picked = [fetch(s, d, pick_sem.at[i]) for i, (s, d) in enumerate(picked)]
    for e in range(experts):
        for f in range(tiles):
            gu_copy(e, f).start()
            if f == 0:
                ga_copy(e).start()
        if e + 1 < experts:
            x_copy(e + 1).start()
        g_copy(e).start()
    slots_of(denseall_ref, me, experts, dense, place)

    def weighed(b, carry):
        weigh(place, dense, weight, b, cap, experts)
        return carry

    lax.fori_loop(0, blocks, weighed, 0)
    for copy in picked:
        copy.wait()

    def expert(e, carry):
        x_copy(e).wait()
        irank[...] = dot(x_rows[e], ha_ref[e], 1, 1).astype(brain)
        ga_copy(e).wait()

        def tile(f, c):
            at = cols(f)
            gu_copy(e, f).wait()
            gate = dot(x_rows[e], gu[e, 0, :, at]) + dot(irank[:, :16], hb_ref[e, 0, :, at])
            up = dot(x_rows[e], gu[e, 1, :, at]) + dot(irank[:, 16:], hb_ref[e, 1, :, at])
            back = ga[e, :, at].astype(single)
            sig = jax.nn.sigmoid(gate)
            swish = gate * sig
            act[e, :, at] = (swish * up).astype(brain)
            gg[:, at] = (back * up * sig * (1.0 + gate * (1.0 - sig))).astype(brain)
            uu[:, at] = (back * swish).astype(brain)
            return c

        lax.fori_loop(0, tiles, tile, 0)
        act_copy(e).start()
        drank_ref[e] = dot(act[e], da_ref[e], 1, 1).astype(brain)
        girank[:, :16] = dot(gg[...], hb_ref[e, 0], 1, 1).astype(brain)
        girank[:, 16:] = dot(uu[...], hb_ref[e, 1], 1, 1).astype(brain)

        def deal(ref, row, value):
            piece = value.shape[1] // replicas
            at = pl.ds(pl.multiple_of(row, 16), value.shape[0])
            for d in range(replicas):
                ref[d, at, :] = value[:, d * piece : (d + 1) * piece].astype(brain)

        deal(gdna_ref, e * 16, dot(gdr_ref[e], act[e], 0, 0))
        deal(gmidb_ref, e * 32, dot(irank[:, :16], gg[...], 0, 0))
        deal(gmidb_ref, e * 32 + 16, dot(irank[:, 16:], uu[...], 0, 0))
        deal(gina_ref, e * 32, dot(girank[...], x_rows[e], 0, 0))
        g_copy(e).wait()
        deal(gdnb_ref, e * 16, dot((drank_ref[e].astype(single) * weight[e]).astype(brain), g_rows[e], 0, 0))

        def slots(d, c):
            at = cols(d)
            s = dot(gg[...], gu[e, 0, at, :], 1, 1) + dot(uu[...], gu[e, 1, at, :], 1, 1)
            s_rows[pl.ds(pl.multiple_of(e * rows, 16), rows), at] = (s + dot(girank[...], ha_ref[e, :, at])).astype(brain)
            return c

        lax.fori_loop(0, width // TILE, slots, 0)
        return carry

    lax.fori_loop(0, experts, expert, 0)
    out_copy = lambda b: pltpu.make_async_copy(out_stage.at[b % 2], gpart_hbm.at[b], out_sem.at[b % 2])

    def combine(b, carry):
        @pl.when(b >= 2)
        def _():
            out_copy(b - 2).wait()

        out_stage[b % 2] = combined(place, s_rows, b, cap, rows)
        out_copy(b).start()
        return carry

    lax.fori_loop(0, blocks, combine, 0)
    for b in (blocks - 2, blocks - 1):
        out_copy(b).wait()
    for e in range(experts):
        act_copy(e).wait()


def moe(ids, dense, gdr, x, g, ga, gu, ha, hb, da, cap, replicas):
    experts, rows, width = x.shape
    blocks, toks = dense.shape[0], dense.shape[2]
    hidden = gu.shape[3]
    rank = da.shape[2]
    vm = pl.BlockSpec(memory_space=pltpu.VMEM)
    sm = pl.BlockSpec(memory_space=pltpu.SMEM)
    hb_ = pl.BlockSpec(memory_space=pl.ANY)
    h = lambda *s: jax.ShapeDtypeStruct(s, brain)
    bv = lambda *s: pltpu.VMEM(s, brain)
    fv = lambda *s: pltpu.VMEM(s, single)
    dma = pltpu.SemaphoreType.DMA
    return pl.pallas_call(
        functools.partial(moe_kernel, cap, replicas),
        out_shape=(
            h(experts, rows, rank),
            h(replicas, experts * 2 * rank, width // replicas), h(replicas, experts * 2 * rank, hidden // replicas),
            h(replicas, experts * rank, hidden // replicas), h(replicas, experts * rank, width // replicas),
            h(blocks, toks, width), h(experts, rows, hidden),
        ),
        in_specs=[sm, vm, vm] + [hb_] * 7,
        out_specs=[vm] * 5 + [hb_] * 2,
        scratch_shapes=[
            bv(*gu.shape), bv(*x.shape), bv(*x.shape), bv(*ga.shape), bv(experts * rows, width), bv(*ga.shape),
            bv(rows, hidden), bv(rows, hidden), fv(blocks * experts, toks), fv(blocks * experts, toks),
            fv(experts, rows, 1), bv(rows, 2 * rank), bv(rows, 2 * rank), bv(experts, 2 * rank, width),
            bv(experts, 2, rank, hidden), bv(experts, rank, hidden), bv(2, toks, width),
            dma((5 * experts,)), dma((experts,)), dma((experts,)), dma((experts,)), dma((experts, hidden // TILE)),
            dma((experts,)), dma((2,)),
        ],
        compiler_params=pltpu.CompilerParams(vmem_limit_bytes=VMEM_ALL),
        name="moe",
    )(ids, dense, gdr, x, g, ga, gu, ha, hb, da)


ADAPTERS = 8
RANK = 16
CLIP = 256.0
beta_one = 0.9
beta_two = 0.95
learn_rate = 0.02
weight_decay = 0.1
adam_eps = 1e-08


def norm_back(values, gain, grad):
    inverse = lax.rsqrt(jnp.mean(values * values, axis=-1, keepdims=True) + norm_eps)
    scaled = grad * gain
    return inverse * scaled - values * (
        inverse * inverse * inverse * jnp.mean(scaled * values, axis=-1, keepdims=True)
    )


def back_kernel(
    cap, replicas,
    ids_ref, hid_ref, top_ref, gain_ref, gain2_ref, low_ref, lse_ref, orank_ref, denseall_ref, drank_ref,
    resid_hbm, seq_hbm, proj_hbm, mixed_hbm, gpart_hbm, act_hbm, dn_hbm, db_hbm,
    w_hbm, a_hbm, b_hbm, wo_hbm, pa_hbm, pb_hbm, gina_hbm, gmidb_hbm, gdna_hbm, gdnb_hbm,
    out_ref, gh_ref, norm_ref, shared_got, got_qb, got_oa, got_ina, got_midb, got_dna, got_dnb,
    resid_ref, proj_ref, mixed_ref, own_g, ypart, act, dn, db_all, part, dense, place, weight,
    w_ref, a_all, b_all, wo_ref, pa_all, pb_all, a_ref,
    bf, gres, gmix, grank, gproj, glow, gk, gv,
    gqb_ref, goa_ref, shared_ref, shared_in, shared_mid, tot_e, tot_d, mine, load_sem, own_sem,
    sh_send, sh_recv, mid_send, mid_recv, p_send, p_recv, t_send, t_recv, *sems,
):
    toks, width = hid_ref.shape
    span = w_ref.shape[2]
    heads = span // HEAD
    n = denseall_ref.shape[0]
    experts = dn.shape[0]
    length = toks * n
    red = Scatter(gpart_hbm, *sems[0:7], own=own_g)
    redy = Scatter(ypart, *sems[7:14])
    redn = Scatter(part, *sems[14:21])
    bf_g = Gather(bf, *sems[21:23])
    me = red.me
    rep = lax.axis_index("dp")
    slot = ids_ref[rep]
    owns = [fetch(gpart_hbm.at[red.order[i]], own_g.at[i], own_sem.at[i]) for i in range(4)]
    loads = {}
    for i, (name, src, dst) in enumerate(
        (
            ("act", act_hbm, act), ("db", db_hbm, db_all), ("dn", dn_hbm, dn), ("resid", resid_hbm, resid_ref), ("wo", wo_hbm, wo_ref), ("pb", pb_hbm, pb_all), ("pa", pa_hbm, pa_all),
            ("mixed", mixed_hbm, mixed_ref), ("proj", proj_hbm, proj_ref), ("b", b_hbm, b_all), ("a", a_hbm, a_all),
            ("w", w_hbm, w_ref), ("ina", gina_hbm.at[rep], got_ina.at[rep]),
            ("midb", gmidb_hbm.at[rep], got_midb.at[rep]), ("dna", gdna_hbm.at[rep], got_dna.at[rep]),
            ("dnb", gdnb_hbm.at[rep], got_dnb.at[rep]),
        )
    ):
        loads[name] = fetch(src, dst, load_sem.at[i])

    def need(*names):
        for name in names:
            loads.pop(name).wait()

    meet(n, replicas, True)
    for i in range(4):
        red.give(i)
    pending = []

    def go(src, dst, send_sem, recv_sem, where):
        copy = pltpu.make_async_remote_copy(
            src_ref=src, dst_ref=dst, send_sem=send_sem, recv_sem=recv_sem, device_id=where
        )
        copy.start()
        pending.append(copy)

    def wait(view, recv_sem):
        pltpu.make_async_remote_copy(
            src_ref=view, dst_ref=view, send_sem=t_send.at[0], recv_sem=recv_sem, device_id={"expert": (me + 1) % n}
        ).wait_recv()

    got = (got_qb, got_oa, got_ina, got_midb, got_dna, got_dnb)

    def swap(i, source):
        for j in range(1, replicas):
            peer = (rep + j) % replicas
            go(
                source.at[peer], got[i].at[rep], p_send.at[i * replicas + j], p_recv.at[i * replicas + rep],
                {"dp": peer},
            )

    def swapped(i):
        for j in range(1, replicas):
            src = (rep + j) % replicas
            wait(got[i].at[src], p_recv.at[i * replicas + src])

    for i, source in enumerate((gina_hbm, gmidb_hbm, gdna_hbm, gdnb_hbm)):
        swap(i + 2, source)
    slots_of(denseall_ref, me, experts, dense, place)

    def weighed(block_at):
        weigh(place, dense, weight, block_at, cap, experts)

    drive(n, weighed, {})
    for copy in owns:
        copy.wait()
    need("act", "db", "dn")
    tiles = width // TILE

    def y_tile(t):
        e = t // tiles
        s = pl.ds(pl.multiple_of(t % tiles * TILE, TILE), TILE)
        y = dot(act[e], dn[e, :, s]) + dot(drank_ref[e], db_all[e, slot, :, s])
        part[pl.ds(pl.multiple_of(e * n * cap, 16), n * cap), s] = (y * weight[e]).astype(brain)

    steps = red.steps()
    drive(
        experts * tiles, y_tile,
        {0: steps[0:1], 1: steps[1:2], 2: steps[2:3], 3: steps[3:4], 6: steps[4:5], 8: steps[5:6], 9: steps[6:7]},
    )
    seq_ref = dn.at[0]
    loads["seq"] = fetch(seq_hbm, seq_ref, load_sem.at[len(loads) + 4])
    need("resid")
    for k in ORDER:
        r = red.rows(k)
        grad = top_ref[r].astype(single) + norm_back(resid_ref[r], gain2_ref[...], red.final(k))
        gres[r] = grad
        bf[me, r] = grad.astype(brain)
        if k != ORDER[0]:
            bf_g.start_own(ORDER[ORDER.index(k) - 1])
    bf_g.start_own(ORDER[-1])
    need("wo", "pb", "pa", "mixed")

    def mixed_grad(block):
        p = block // 2
        both = bf[pl.ds(2 * p, 2)].reshape(2 * toks, width)
        at = two(p, toks)
        rank = dot(both, pb_all[slot], 1, 1).astype(brain)
        grank[at, :] = rank
        gmix[at, :] = (dot(both, wo_ref[...], 1, 1) + dot(rank, pa_all[slot])).astype(brain)

    def y_block(block_at):
        ypart[block_at] = combined(place, part, block_at, cap, n * cap)

    bf_g.pair(me)
    mixed_grad(me)
    drive(
        n, y_block, {2: [functools.partial(bf_g.relay, 0)], 6: [functools.partial(bf_g.relay, 1)]},
    )
    for i in range(2, CHUNKS):
        bf_g.relay(i)
    for i in range(4):
        redy.give(i)
    bf_g.pair(bf_g.across)
    mixed_grad(bf_g.across)
    for i in range(CHUNKS // 2):
        bf_g.relay_far(i)
    bf_g.pair(bf_g.along)
    mixed_grad(bf_g.along)
    bf_g.pair(bf_g.far)
    mixed_grad(bf_g.far)

    piece = span // replicas
    goa = dot(grank[...], mixed_ref[...], 0, 0)
    for d in range(replicas):
        goa_ref[d] = goa[:, d * piece : (d + 1) * piece].astype(brain)
    got_oa[rep] = goa_ref[rep]
    swap(1, goa_ref)

    need("proj")
    steps = redy.steps()
    scale = HEAD ** (-0.5)
    block = 256
    for h in range(heads):
        at = slice(h * HEAD, (h + 1) * HEAD)
        gk[...] = jnp.zeros_like(gk)
        gv[...] = jnp.zeros_like(gv)

        def attend(i, h=h, at=at):
            r = pl.ds(pl.multiple_of(i * block, block), block)
            q, do = proj_ref[0, r, at], gmix[r, at]
            delta = jnp.sum(do.astype(single) * mixed_ref[r, at].astype(single), axis=-1, keepdims=True)
            probs = jnp.exp(dot(q, proj_ref[1, :, at], 1, 1) * scale - lse_ref[r, h : h + 1])
            gp = dot(do, proj_ref[2, :, at], 1, 1)
            gs = (probs * (gp - delta)).astype(brain)
            gproj[0, r, at] = (dot(gs, proj_ref[1, :, at]) * scale).astype(brain)
            gk[...] += dot(gs, q, 0, 0)
            gv[...] += dot(probs.astype(brain), do, 0, 0)

        count = (len(steps) + heads - 1) // heads
        mine_now = steps[h * count : (h + 1) * count]
        drive(length // block, attend, {i: mine_now[i : i + 1] for i in range(len(mine_now))})
        gproj[1, :, at] = (gk[...] * scale).astype(brain)
        gproj[2, :, at] = gv[...].astype(brain)

    need("a", "b", "w")
    for j in range(3):
        a_ref[16 * j : 16 * j + 16, :] = a_all[j, slot]
    for i in range(4):
        p = redn.order[i] // 2
        at = two(p, toks)
        for j in range(3):
            glow[at, 16 * j : 16 * j + 16] = dot(gproj[j, at, :], b_all[j, slot], 1, 1).astype(brain)
        wide = min(1024, width)

        def normed_grad(c, carry, p=p, at=at):
            s = pl.ds(pl.multiple_of(c * wide, wide), wide)
            out = dot(glow[at, :], a_ref[:, s])
            for j in range(3):
                out = out + dot(gproj[j, at, :], w_ref[j, s, :], 1, 1)
            part[at, s] = out.astype(brain)
            return carry

        lax.fori_loop(0, width // wide, normed_grad, 0)
        if i:
            redn.give(i - 1)
    redn.give(3)

    thin = width // (n * replicas)

    def share(row, value, base):
        for c in range(value.shape[1] // thin):
            d, e = (base + c) // n, (base + c) % n
            shared_ref[e, row : row + value.shape[0], d * thin : (d + 1) * thin] = value[
                :, c * thin : (c + 1) * thin
            ].astype(brain)

    nsteps = redn.steps()

    def advance():
        if nsteps:
            nsteps.pop(0)()

    for j in range(3):
        gqb = dot(low_ref[:, 16 * j : 16 * j + 16], gproj[j], 0, 0)
        for d in range(replicas):
            gqb_ref[d, 16 * j : 16 * j + 16, :] = gqb[:, d * piece : (d + 1) * piece].astype(brain)
    advance()
    got_qb[rep] = gqb_ref[rep]
    swap(0, gqb_ref)
    need("seq")
    cols = 512
    for c in range(width // cols):
        s = slice(c * cols, (c + 1) * cols)
        share(0, dot(glow[...], seq_ref[:, s], 0, 0), c * cols // thin)
        share(48, dot(orank_ref[...], bf[:, :, s].reshape(length, cols), 0, 0), c * cols // thin)
        advance()
    shared_in[me] = shared_ref[me]
    for j in range(1, n):
        peer = (me + j) % n
        go(shared_ref.at[peer], shared_in.at[me], sh_send.at[j - 1], sh_recv.at[me], {"expert": peer})
    while nsteps:
        advance()

    def squares(i, source):
        rows = source.shape[1] // RANK

        def body(t, acc):
            at = pl.ds(pl.multiple_of(t // ADAPTERS * RANK, RANK), RANK)
            value = jnp.zeros((RANK, source.shape[2]), single)
            for s in range(replicas):
                value = value + source[s, at, :].astype(single) * jnp.where(ids_ref[s] == t % ADAPTERS, 1.0, 0.0)
            return acc + value * value

        return jnp.sum(
            lax.fori_loop(0, rows * ADAPTERS, body, jnp.zeros((RANK, source.shape[2]), single))
        )

    need("ina", "midb", "dna", "dnb")
    total = jnp.zeros((), single)
    for i in range(2, 6):
        swapped(i)
        total = total + squares(i, got[i])
    for j in range(1, n):
        src = (me + j) % n
        wait(shared_in.at[src], sh_recv.at[src])
    summed = shared_in[0].astype(single)
    for e in range(1, n):
        summed = summed + shared_in[e].astype(single)
    for d in range(replicas):
        shared_mid[d] = summed[:, d * thin : (d + 1) * thin].astype(brain)
    shared_got[rep] = shared_mid[rep]
    for j in range(1, replicas):
        peer = (rep + j) % replicas
        go(shared_mid.at[peer], shared_got.at[rep], mid_send.at[j], mid_recv.at[rep], {"dp": peer})
    for k in ORDER:
        r = redy.rows(k)
        out_ref[r] = (resid_ref[r] + redy.final(k)).astype(brain)
    for i in range(2):
        swapped(i)
        total = total + squares(i, got[i])
    for j in range(1, replicas):
        src = (rep + j) % replicas
        wait(shared_got.at[src], mid_recv.at[src])
    total = total + squares(0, shared_got)

    mine[0] = jnp.full(mine.shape[1:], total, single)
    tot_e[me] = mine[0]
    for j in range(1, n):
        go(mine.at[0], tot_e.at[me], t_send.at[j], t_recv.at[me], {"expert": (me + j) % n})
    for j in range(1, n):
        src = (me + j) % n
        wait(tot_e.at[src], t_recv.at[src])
    total = tot_e[0]
    for e in range(1, n):
        total = total + tot_e[e]
    mine[1] = total
    tot_d[rep] = mine[1]
    for j in range(1, replicas):
        go(mine.at[1], tot_d.at[rep], t_send.at[n + j], t_recv.at[n + rep], {"dp": (rep + j) % replicas})
    for k in ORDER:
        r = redn.rows(k)
        gh_ref[r] = gres[r] + norm_back(hid_ref[r].astype(single), gain_ref[...], redn.final(k))
    for j in range(1, replicas):
        src = (rep + j) % replicas
        wait(tot_d.at[src], t_recv.at[n + src])
    total = tot_d[0]
    for d in range(1, replicas):
        total = total + tot_d[d]
    norm_ref[...] = jnp.sqrt(total)
    for mover in (red, redy, redn, bf_g):
        mover.drain()
    for copy in pending:
        copy.wait_send()


def back(
    ids, hid, top, gain, gain2, low, lse, orank, dense, drank, resid, seq, proj, mixed, gpart, act, dn, db,
    w, a, b, wo, pa, pb, pieces, cap, replicas, cid=1,
):
    n, toks, width = seq.shape
    seq = seq.reshape(n * toks, width)
    experts, rows = act.shape[:2]
    span = w.shape[2]
    length = toks * n
    vm = pl.BlockSpec(memory_space=pltpu.VMEM)
    sm = pl.BlockSpec(memory_space=pltpu.SMEM)
    hb = pl.BlockSpec(memory_space=pl.ANY)
    f = lambda *s: jax.ShapeDtypeStruct(s, single)
    h = lambda *s: jax.ShapeDtypeStruct(s, brain)
    bv = lambda *s: pltpu.VMEM(s, brain)
    fv = lambda *s: pltpu.VMEM(s, single)
    dma = pltpu.SemaphoreType.DMA
    thin = width // (n * replicas)
    piece = span // replicas
    return pl.pallas_call(
        functools.partial(back_kernel, cap, replicas),
        out_shape=(
            h(toks, width), f(toks, width), f(8, 128), h(replicas, 64, thin), h(replicas, 48, piece),
            h(replicas, 16, piece),
        ) + tuple(h(*p.shape) for p in pieces),
        in_specs=[sm] + [vm] * 9 + [hb] * 18,
        out_specs=[vm] * 10,
        scratch_shapes=[
            fv(toks, width), bv(3, length, span), bv(length, span), bv(4, toks, width), bv(n, toks, width),
            bv(*act.shape), bv(*dn.shape), bv(*db.shape), bv(experts * rows, width), fv(n * experts, toks),
            fv(n * experts, toks), fv(experts, rows, 1),
        ]
        + [pltpu.VMEM(v.shape, brain) for v in (w, a, b, wo, pa, pb)]
        + [
            bv(48, width), bv(n, toks, width), fv(toks, width), bv(length, span), bv(length, 16),
            bv(3, length, span), bv(length, 48), fv(length, HEAD), fv(length, HEAD),
            bv(replicas, 48, piece), bv(replicas, 16, piece), bv(n, 64, replicas * thin), bv(n, 64, replicas * thin),
            bv(replicas, 64, thin), fv(n, 8, 128), fv(replicas, 8, 128), fv(2, 8, 128), dma((20,)), dma((4,)),
            dma((n,)), dma((n,)), dma((replicas,)), dma((replicas,)), dma((6 * replicas,)), dma((6 * replicas,)),
            dma((n + replicas,)), dma((n + replicas,)),
        ]
        + scatter_scratch(toks, width) * 3 + gather_scratch(n),
        compiler_params=pltpu.CompilerParams(collective_id=cid, has_side_effects=True, vmem_limit_bytes=VMEM_ALL),
        name="back",
    )(
        ids, hid, top, gain, gain2, low, lse, orank, dense, drank, resid, seq, proj, mixed, gpart, act, dn, db,
        w, a, b, wo, pa, pb, *pieces,
    )


def adam_kernel(n, replicas, groups, spans, adapter_ref, step_ref, norm_in, out_in, gh_in, *refs):
    got, refs = refs[:7], refs[7:]
    weight_hbm, first_hbm, second_hbm, refs = refs[:8], refs[8:16], refs[16:24], refs[24:]
    out_hbm, gh_hbm, norm_ref, result, refs = refs[0], refs[1], refs[2], refs[3:35], refs[35:]
    weight, first, second, kept, refs = refs[:8], refs[8:16], refs[16:24], refs[24:56], refs[56:]
    load_sem, save_sem = refs
    me, rep = lax.axis_index("expert"), lax.axis_index("dp")
    common = rep * n + me
    loads, saves = [], []
    for a in range(8):
        size, pieces = spans[a]
        index = common if pieces == n * replicas else rep
        start = index * size // weight[a].shape[1] * weight[a].shape[1]
        view = weight_hbm[a].at[:, pl.ds(pl.multiple_of(start, 128), weight[a].shape[1])]
        loads.append(
            [
                fetch(src, dst, load_sem.at[3 * a + k])
                for k, (src, dst) in enumerate(((view, weight[a]), (first_hbm[a], first[a]), (second_hbm[a], second[a])))
            ]
        )
    saves.append(fetch(out_in, out_hbm, save_sem.at[32]))
    saves.append(fetch(gh_in, gh_hbm, save_sem.at[33]))
    norm_ref[0] = norm_in[0, 0]
    factor = jnp.minimum(1.0, CLIP / norm_in[...])[0:1, 0:1]
    steps = jnp.full((8, 128), step_ref[0].astype(single), single)
    fix_first = (1.0 / (1.0 - jnp.exp(steps * jnp.log(jnp.full((8, 128), beta_one, single)))))[0:1, 0:1]
    fix_second = (1.0 / (1.0 - jnp.exp(steps * jnp.log(jnp.full((8, 128), beta_two, single)))))[0:1, 0:1]
    for a in (4, 7, 5, 6, 0, 2, 1, 3):
        for copy in loads[a]:
            copy.wait()
        source = got[max(a - 1, 0)]
        base = groups[0] if a == 1 else 0
        size, pieces = spans[a]
        window = weight[a].shape[1]
        index = common if pieces == n * replicas else rep

        def body(t, carry, a=a, source=source, base=base, size=size, window=window, index=index):
            rows = pl.ds(pl.multiple_of((base + t) * RANK, RANK), RANK)
            parts = [source[s, rows, :].astype(single) for s in range(replicas)]
            for adapter in range(ADAPTERS):
                at = pl.ds(pl.multiple_of((t * ADAPTERS + adapter) * RANK, RANK), RANK)
                grad = jnp.zeros((RANK, size), single)
                for s in range(replicas):
                    grad = grad + parts[s] * jnp.where(adapter_ref[s] == adapter, 1.0, 0.0)
                held = weight[a][at, :].astype(single)
                w = held[:, :size]
                for c in range(1, window // size):
                    w = jnp.where(index % (window // size) == c, held[:, c * size : (c + 1) * size], w)
                clipped = grad * factor
                f = beta_one * first[a][at, :] + (1.0 - beta_one) * clipped
                s = beta_two * second[a][at, :] + (1.0 - beta_two) * clipped * clipped
                kept[4 * a][at, :] = grad
                kept[4 * a + 1][at, :] = f
                kept[4 * a + 2][at, :] = s
                kept[4 * a + 3][at, :] = -learn_rate * (
                    f * fix_first / (jnp.sqrt(s * fix_second) + adam_eps) + weight_decay * w
                )
            return carry

        lax.fori_loop(0, groups[a], body, 0)
        for k in range(4):
            saves.append(fetch(kept[4 * a + k], result[4 * a + k], save_sem.at[4 * a + k]))
    for copy in saves:
        copy.wait()


def adam(adapters, steps, norm, block_out, gh, got, weight, pieces, first, second, n, replicas):
    spans = tuple((f.shape[1], p) for f, p in zip(first, pieces))
    groups = tuple(f.shape[0] // (ADAPTERS * RANK) for f in first)
    vm = pl.BlockSpec(memory_space=pltpu.VMEM)
    sm = pl.BlockSpec(memory_space=pltpu.SMEM)
    hb = pl.BlockSpec(memory_space=pl.ANY)
    f = lambda s: jax.ShapeDtypeStruct(s, single)
    dma = pltpu.SemaphoreType.DMA
    shapes = [t.shape for t in first]
    return pl.pallas_call(
        functools.partial(adam_kernel, n, replicas, groups, spans),
        out_shape=(jax.ShapeDtypeStruct(block_out.shape, brain), f(gh.shape), f((1,)))
        + tuple(f(s) for s in shapes for _ in range(4)),
        in_specs=[sm, sm, vm, vm, vm] + [vm] * 7 + [hb] * 24,
        out_specs=[hb, hb, sm] + [hb] * 32,
        scratch_shapes=[pltpu.VMEM((s[0], max(s[1], 128)), brain) for s in shapes]
        + [pltpu.VMEM(s, single) for s in shapes] * 2
        + [pltpu.VMEM(s, single) for s in shapes for _ in range(4)]
        + [dma((24,)), dma((34,))],
        compiler_params=pltpu.CompilerParams(vmem_limit_bytes=VMEM_ALL),
        name="adam",
    )(adapters, steps, norm, block_out, gh, *got, *weight, *first, *second)


def per_device(
    hidden,
    output_cotangent,
    attention_gain,
    expert_norm_gain,
    query_key_value_weight,
    output_weight,
    gate_up_weight,
    down_weight,
    token_experts,
    expert_gate_weight,
    sequence_adapter,
    optimizer_steps,
    adapter_attention_input,
    adapter_attention_output,
    adapter_projection_input,
    adapter_projection_output,
    adapter_hidden_input,
    adapter_hidden_output,
    adapter_down_input,
    adapter_down_output,
    moment_attention_input,
    moment_attention_output,
    moment_projection_input,
    moment_projection_output,
    moment_hidden_input,
    moment_hidden_output,
    moment_down_input,
    moment_down_output,
    squared_attention_input,
    squared_attention_output,
    squared_projection_input,
    squared_projection_output,
    squared_hidden_input,
    squared_hidden_output,
    squared_down_input,
    squared_down_output,
):
    n = lax.axis_size("expert")
    replicas = lax.axis_size("dp")
    toks, width = hidden.shape[1:]
    here = down_weight.shape[0]
    cap = min(toks, toks * token_experts.shape[2] * 5 // (4 * here * n))
    gain = attention_gain[None]
    gain2 = expert_norm_gain[None]
    hid, cot = hidden[0], output_cotangent[0]
    low, lse, dense_all, orank, gdr, seq, proj, mixed, resid, x_rows, g_rows, ga = front(
        sequence_adapter, hid, cot, token_experts[0].T, expert_gate_weight[0].T, gain, gain2, query_key_value_weight,
        adapter_attention_input, adapter_attention_output, output_weight, adapter_projection_input,
        adapter_projection_output, down_weight, adapter_down_input, adapter_down_output, n, cap,
    )
    drank, *pieces, gpart, act = moe(
        sequence_adapter, dense_all, gdr, x_rows, g_rows, ga, gate_up_weight, adapter_hidden_input,
        adapter_hidden_output, adapter_down_input, cap, replicas,
    )
    block_out, grad_hidden, norm, *got = back(
        sequence_adapter, hid, cot, gain, gain2, low, lse, orank, dense_all, drank, resid, seq, proj, mixed, gpart,
        act, down_weight, adapter_down_output,
        query_key_value_weight, adapter_attention_input, adapter_attention_output, output_weight,
        adapter_projection_input, adapter_projection_output, tuple(pieces), cap, replicas,
    )

    def flat(array):
        return array.reshape(-1, array.shape[-1])

    weights = (
        adapter_attention_input, adapter_projection_output, adapter_attention_output, adapter_projection_input,
        adapter_hidden_input, adapter_hidden_output, adapter_down_input, adapter_down_output,
    )
    first = (
        moment_attention_input, moment_projection_output, moment_attention_output, moment_projection_input,
        moment_hidden_input, moment_hidden_output, moment_down_input, moment_down_output,
    )
    second = (
        squared_attention_input, squared_projection_output, squared_attention_output, squared_projection_input,
        squared_hidden_input, squared_hidden_output, squared_down_input, squared_down_output,
    )
    outs = adam(
        sequence_adapter, optimizer_steps, norm, block_out, grad_hidden, got, tuple(flat(w) for w in weights),
        (n * replicas,) * 2 + (replicas,) * 6, tuple(flat(m) for m in first), tuple(flat(s) for s in second),
        n, replicas,
    )
    results = [outs[0][None], outs[1][None], outs[2]]
    for a in (0, 2, 3, 1, 4, 5, 6, 7):
        for kind in range(4):
            results.append(outs[3 + 4 * a + kind].reshape(first[a].shape))
    return tuple(results)


def solution(mesh):
    return jax.shard_map(
        per_device,
        mesh=mesh,
        in_specs=(
            P("dp", "expert", None),
            P("dp", "expert", None),
            P(),
            P(),
            P(None, None, "expert"),
            P("expert", None),
            P("expert", None, None, None),
            P("expert", None, None),
            P("dp", "expert", None),
            P("dp", "expert", None),
            P(),
            P(),
            P(),
            P(None, None, None, "expert"),
            P(None, None, "expert"),
            P(),
            P("expert", None, None, None, None),
            P("expert", None, None, None, None),
            P("expert", None, None, None),
            P("expert", None, None, None),
            P(None, None, None, ("dp", "expert")),
            P(None, None, None, ("expert", "dp")),
            P(None, None, ("expert", "dp")),
            P(None, None, ("dp", "expert")),
            P("expert", None, None, None, "dp"),
            P("expert", None, None, None, "dp"),
            P("expert", None, None, "dp"),
            P("expert", None, None, "dp"),
            P(None, None, None, ("dp", "expert")),
            P(None, None, None, ("expert", "dp")),
            P(None, None, ("expert", "dp")),
            P(None, None, ("dp", "expert")),
            P("expert", None, None, None, "dp"),
            P("expert", None, None, None, "dp"),
            P("expert", None, None, "dp"),
            P("expert", None, None, "dp"),
        ),
        out_specs=(
            P("dp", "expert", None),
            P("dp", "expert", None),
            P(),
            P(None, None, None, ("dp", "expert")),
            P(None, None, None, ("dp", "expert")),
            P(None, None, None, ("dp", "expert")),
            P(None, None, None, ("dp", "expert")),
            P(None, None, None, ("expert", "dp")),
            P(None, None, None, ("expert", "dp")),
            P(None, None, None, ("expert", "dp")),
            P(None, None, None, ("expert", "dp")),
            P(None, None, ("expert", "dp")),
            P(None, None, ("expert", "dp")),
            P(None, None, ("expert", "dp")),
            P(None, None, ("expert", "dp")),
            P(None, None, ("dp", "expert")),
            P(None, None, ("dp", "expert")),
            P(None, None, ("dp", "expert")),
            P(None, None, ("dp", "expert")),
            P("expert", None, None, None, "dp"),
            P("expert", None, None, None, "dp"),
            P("expert", None, None, None, "dp"),
            P("expert", None, None, None, "dp"),
            P("expert", None, None, None, "dp"),
            P("expert", None, None, None, "dp"),
            P("expert", None, None, None, "dp"),
            P("expert", None, None, None, "dp"),
            P("expert", None, None, "dp"),
            P("expert", None, None, "dp"),
            P("expert", None, None, "dp"),
            P("expert", None, None, "dp"),
            P("expert", None, None, "dp"),
            P("expert", None, None, "dp"),
            P("expert", None, None, "dp"),
            P("expert", None, None, "dp"),
        ),
        check_vma=False,
    )
```

profile of v0, /device:TPU:0, one launch (start us, length us, event | category | flops | bytes accessed | tf_op | source)
XLA Modules:
  0.0 258.9 jit_solution(5754023535659023655)
XLA Ops:
  0.7 89.4 %front.1 = (bf16[1024,48]{1,0:T(8,128)(2,1)}, f32[1024,2]{1,0:T(8,128)}, f32[8,16,128]{2,1,0:T(8,128)}, bf16[1024,16]{1,0:T(8,128)(2,1)}, bf16[2,640,16]{2,1,0:T...) custom-call(s32[4]{0:T(128)} %adapter_ref.1, ...), custom_call_target="tpu_custom_call" | custom-call | tf_op jit(solution)/shard_map/front/pallas_call | solution.py:538
  90.1 51.3 %moe.1 = (bf16[2,640,16]{2,1,0:T(8,128)(2,1)}, bf16[4,64,512]{2,1,0:T(8,128)(2,1)}, bf16[4,64,256]{2,1,0:T(8,128)(2,1)}, bf16[4,32,256]{2,1,0:T(8,128)(2,1)}, bf...) custom-call(s32[4]{0:T(128)} %adapter_ref.1, ...), custom_call_target="tpu_custom_call" | custom-call | tf_op jit(solution)/shard_map/moe/pallas_call | solution.py:689
  141.4 105.7 %back.1 = (bf16[128,2048]{1,0:T(8,128)(2,1)}, f32[128,2048]{1,0:T(8,128)}, f32[8,128]{1,0:T(8,128)}, bf16[4,64,64]{2,1,0:T(8,128)(2,1)}, bf16[4,48,64]{2,1,0:T(8...) custom-call(s32[4]{0:T(128)} %adapter_ref.1, ...), custom_call_target="tpu_custom_call" | custom-call | tf_op jit(solution)/shard_map/back/pallas_call | solution.py:1053
  247.8 11.0 %adam.1 = (bf16[128,2048]{1,0:T(8,128)(2,1)}, f32[128,2048]{1,0:T(8,128)}, f32[1]{0:T(128)}, f32[384,64]{1,0:T(8,128)}, f32[384,64]{1,0:T(8,128)}, /*index=5*/f3...) custom-call(s32[4]{0:T(128)} %adapter_ref.1, ...), custom_call_target="tpu_custom_call" | custom-call | tf_op jit(solution)/shard_map/adam/pallas_call | solution.py:1159
where the time goes:
time: 259 us
  Pallas kernels  257 us (99%)
    pallas_call x1, Pallas kernels, back(): pl.pallas_call(functools.partial(back_kernel, cap, replicas), out_shape=(...  106 us
    pallas_call x1, Pallas kernels, front(): pl.pallas_call(functools.partial(front_kernel, cap), out_shape=(h(length,...  89.4 us
    pallas_call x1, Pallas kernels, moe(): pl.pallas_call(functools.partial(moe_kernel, cap, replicas), out_shape=(h...  51.3 us
    pallas_call x1, Pallas kernels, adam(): pl.pallas_call(functools.partial(adam_kernel, n, replicas, groups, spans)...  11 us

commit v1 on v0

--- a/solution.py
+++ b/solution.py
@@ -316,9 +316,9 @@
 def front_kernel(
     cap, ids_ref, hid_ref, top_ref, routes_ref, gates_ref, gain_ref, gain2_ref,
     w_hbm, a_hbm, b_hbm, wo_hbm, pa_hbm, pb_hbm, dn_hbm, da_hbm, db_hbm,
-    low_ref, lse_ref, denseall_ref, orank_ref, gdr_ref, seq_hbm, proj_hbm, mixed_hbm, resid_hbm, x_hbm, g_hbm, ga_hbm,
+    low_ref, lse_ref, orank_ref, gdr_ref, place, weight, seq_hbm, proj_hbm, mixed_hbm, resid_hbm, x_hbm, g_hbm, ga_hbm,
     part, seq_ref, proj_ref, mixed_ref, topseq_ref, resid_ref, moe_ref, x_rows, g_rows, ga,
-    w_ref, a_all, b_all, wo_ref, pa_all, pb_all, dn, da_all, db_all, a_ref, b_ref, mydense, dense, place, weight,
+    w_ref, a_all, b_all, wo_ref, pa_all, pb_all, dn, da_all, db_all, a_ref, b_ref, mydense, dense, denseall_ref,
     load_sem, save_sem, *sems,
 ):
     toks, width = hid_ref.shape
@@ -393,10 +393,11 @@
     top_g.start()
     seq_g.pair(seq_g.across)
     qkv(seq_g.across)
-    for i in range(CHUNKS // 2):
-        seq_g.relay_far(i)
+    seq_g.relay_far(0)
     seq_g.pair(seq_g.along)
     qkv(seq_g.along)
+    for i in range(1, CHUNKS // 2):
+        seq_g.relay_far(i)
     seq_g.pair(seq_g.far)
     qkv(seq_g.far)
     save(seq_ref, seq_hbm)
@@ -420,8 +421,11 @@
             mixed_ref[r, at] = dot(probs, proj_ref[2, :, at]).astype(brain)
             lse_ref[r, h : h + 1] = peak + jnp.log(total)
 
-        drive(length // block, attend, {1: top_steps[3 * h : 3 * h + 1], 3: top_steps[3 * h + 1 : 3 * h + 3]})
-    del top_steps[: 3 * heads]
+        now, top_steps = top_steps[:3], top_steps[3:]
+        last = length // block - 1
+        drive(length // block, attend, {0: now[:1], last - 1: now[1:2], last: now[2:]} if h == 0 else {1: now[:1]})
+        if h:
+            top_steps = now[1:] + top_steps
     for copy in loads[3:6]:
         copy.wait()
 
@@ -443,6 +447,11 @@
             red.give(i - 1)
     red.give(3)
     save(mixed_ref, mixed_hbm)
+    steps = red.steps()
+    for step in steps[:4]:
+        step()
+    top_steps.pop(0)()
+    red.flush()
     for step in top_steps:
         step()
     for block_at in (me, top_g.across, top_g.along, top_g.far):
@@ -456,13 +465,12 @@
     for j in range(1, n):
         dense_copy(j).wait_send()
     slots_of(denseall_ref, me, experts, dense, place)
-    steps = red.steps()
 
     def top_rows(b):
         weigh(place, dense, weight, b, cap, experts)
         take(place, topseq_ref[b], g_rows, b, cap)
 
-    drive(n, top_rows, {1: steps[0:1], 2: steps[1:2], 3: steps[2:3], 4: steps[3:4]})
+    drive(n, top_rows, {5: steps[4:5]})
     for copy in loads[6:]:
         copy.wait()
 
@@ -480,7 +488,7 @@
         out = dot(g_rows[e, r, :], dn[e, at, :], 1, 1) * weight[e, r, :]
         ga[e, r, at] = (out + dot(gdr_ref[e, r, :], da_all[e, slot, :, at])).astype(brain)
 
-    drive(2 * experts * tiles, top_tile, {2: steps[4:5], 4: steps[5:6], 5: steps[6:7]})
+    drive(2 * experts * tiles, top_tile, {0: steps[5:6], 1: steps[6:7]})
     save(g_rows, g_hbm)
     save(ga, ga_hbm)
     for k in ORDER:
@@ -538,20 +546,21 @@
     return pl.pallas_call(
         functools.partial(front_kernel, cap),
         out_shape=(
-            h(length, 48), f(length, span // HEAD), f(n, experts * n, toks), h(length, 16), h(experts, rows, 16),
+            h(length, 48), f(length, span // HEAD), h(length, 16), h(experts, rows, 16), f(n * experts, toks),
+            f(experts, rows, 1),
             h(n, toks, width), h(3, length, span), h(length, span), f(toks, width),
             h(experts, rows, width), h(experts, rows, width), h(experts, rows, hidden),
         ),
         in_specs=[sm] + [vm] * 6 + [hb] * 9,
-        out_specs=[vm] * 5 + [hb] * 7,
+        out_specs=[vm] * 6 + [hb] * 7,
         scratch_shapes=[
             whole, whole, bv(3, length, span), bv(length, span), whole, fv(toks, width), whole,
             bv(experts, rows, width), bv(experts, rows, width), bv(experts, rows, hidden),
         ]
         + [pltpu.VMEM(v.shape, brain) for v in (w, a, b, wo, pa, pb, dn, da, db)]
         + [
-            bv(48, width), bv(3, 48, span), fv(experts * n, toks), fv(n * experts, toks), fv(n * experts, toks),
-            fv(experts, rows, 1), pltpu.SemaphoreType.DMA((9,)), pltpu.SemaphoreType.DMA((7,)),
+            bv(48, width), bv(3, 48, span), fv(experts * n, toks), fv(n * experts, toks), fv(n, experts * n, toks),
+            pltpu.SemaphoreType.DMA((9,)), pltpu.SemaphoreType.DMA((7,)),
         ]
         + gather_scratch(n) + gather_scratch(n) + gather_scratch(n) + scatter_scratch(toks, width)
         + [pltpu.SemaphoreType.DMA((n,)), pltpu.SemaphoreType.DMA((n,))],
@@ -561,16 +570,15 @@
 
 
 def moe_kernel(
-    cap, replicas, ids_ref, denseall_ref, gdr_ref, x_hbm, g_hbm, ga_hbm, gu_hbm, ha_hbm, hb_hbm, da_hbm,
+    cap, replicas, ids_ref, place, weight, gdr_ref, x_hbm, g_hbm, ga_hbm, gu_hbm, ha_hbm, hb_hbm, da_hbm,
     drank_ref, gina_ref, gmidb_ref, gdna_ref, gdnb_ref, gpart_hbm, act_hbm,
-    gu, x_rows, g_rows, ga, s_rows, act, gg, uu, dense, place, weight, irank, girank, ha_ref, hb_ref, da_ref,
+    gu, x_rows, g_rows, ga, s_rows, act, gg, uu, irank, girank, ha_ref, hb_ref, da_ref,
     out_stage, pick_sem, x_sem, g_sem, ga_sem, gu_sem, act_sem, out_sem,
 ):
     experts, width, hidden = gu.shape[0], gu.shape[2], gu.shape[3]
-    blocks = denseall_ref.shape[0]
+    blocks = place.shape[0] // experts
     rows = x_rows.shape[1]
     tiles = hidden // TILE
-    me = lax.axis_index("expert")
     which = ids_ref[lax.axis_index("dp")]
     picked = []
     for e in range(experts):
@@ -599,13 +607,6 @@
         if e + 1 < experts:
             x_copy(e + 1).start()
         g_copy(e).start()
-    slots_of(denseall_ref, me, experts, dense, place)
-
-    def weighed(b, carry):
-        weigh(place, dense, weight, b, cap, experts)
-        return carry
-
-    lax.fori_loop(0, blocks, weighed, 0)
     for copy in picked:
         copy.wait()
 
@@ -674,9 +675,9 @@
         act_copy(e).wait()
 
 
-def moe(ids, dense, gdr, x, g, ga, gu, ha, hb, da, cap, replicas):
+def moe(ids, place, weight, gdr, x, g, ga, gu, ha, hb, da, cap, replicas):
     experts, rows, width = x.shape
-    blocks, toks = dense.shape[0], dense.shape[2]
+    blocks, toks = place.shape[0] // experts, place.shape[1]
     hidden = gu.shape[3]
     rank = da.shape[2]
     vm = pl.BlockSpec(memory_space=pltpu.VMEM)
@@ -694,19 +695,18 @@
             h(replicas, experts * rank, hidden // replicas), h(replicas, experts * rank, width // replicas),
             h(blocks, toks, width), h(experts, rows, hidden),
         ),
-        in_specs=[sm, vm, vm] + [hb_] * 7,
+        in_specs=[sm, vm, vm, vm] + [hb_] * 7,
         out_specs=[vm] * 5 + [hb_] * 2,
         scratch_shapes=[
             bv(*gu.shape), bv(*x.shape), bv(*x.shape), bv(*ga.shape), bv(experts * rows, width), bv(*ga.shape),
-            bv(rows, hidden), bv(rows, hidden), fv(blocks * experts, toks), fv(blocks * experts, toks),
-            fv(experts, rows, 1), bv(rows, 2 * rank), bv(rows, 2 * rank), bv(experts, 2 * rank, width),
+            bv(rows, hidden), bv(rows, hidden), bv(rows, 2 * rank), bv(rows, 2 * rank), bv(experts, 2 * rank, width),
             bv(experts, 2, rank, hidden), bv(experts, rank, hidden), bv(2, toks, width),
             dma((5 * experts,)), dma((experts,)), dma((experts,)), dma((experts,)), dma((experts, hidden // TILE)),
             dma((experts,)), dma((2,)),
         ],
         compiler_params=pltpu.CompilerParams(vmem_limit_bytes=VMEM_ALL),
         name="moe",
-    )(ids, dense, gdr, x, g, ga, gu, ha, hb, da)
+    )(ids, place, weight, gdr, x, g, ga, gu, ha, hb, da)
 
 
 ADAPTERS = 8
@@ -729,11 +729,11 @@
 
 def back_kernel(
     cap, replicas,
-    ids_ref, hid_ref, top_ref, gain_ref, gain2_ref, low_ref, lse_ref, orank_ref, denseall_ref, drank_ref,
+    ids_ref, hid_ref, top_ref, gain_ref, gain2_ref, low_ref, lse_ref, orank_ref, place, weight, drank_ref,
     resid_hbm, seq_hbm, proj_hbm, mixed_hbm, gpart_hbm, act_hbm, dn_hbm, db_hbm,
     w_hbm, a_hbm, b_hbm, wo_hbm, pa_hbm, pb_hbm, gina_hbm, gmidb_hbm, gdna_hbm, gdnb_hbm,
     out_ref, gh_ref, norm_ref, shared_got, got_qb, got_oa, got_ina, got_midb, got_dna, got_dnb,
-    resid_ref, proj_ref, mixed_ref, own_g, ypart, act, dn, db_all, part, dense, place, weight,
+    resid_ref, proj_ref, mixed_ref, own_g, ypart, act, dn, db_all, part,
     w_ref, a_all, b_all, wo_ref, pa_all, pb_all, a_ref,
     bf, gres, gmix, grank, gproj, glow, gk, gv,
     gqb_ref, goa_ref, shared_ref, shared_in, shared_mid, tot_e, tot_d, mine, load_sem, own_sem,
@@ -742,8 +742,8 @@
     toks, width = hid_ref.shape
     span = w_ref.shape[2]
     heads = span // HEAD
-    n = denseall_ref.shape[0]
     experts = dn.shape[0]
+    n = place.shape[0] // experts
     length = toks * n
     red = Scatter(gpart_hbm, *sems[0:7], own=own_g)
     redy = Scatter(ypart, *sems[7:14])
@@ -801,16 +801,14 @@
             src = (rep + j) % replicas
             wait(got[i].at[src], p_recv.at[i * replicas + src])
 
+    for copy in owns:
+        copy.wait()
+    steps = red.steps()
+    for step in steps[:4]:
+        step()
     for i, source in enumerate((gina_hbm, gmidb_hbm, gdna_hbm, gdnb_hbm)):
         swap(i + 2, source)
-    slots_of(denseall_ref, me, experts, dense, place)
-
-    def weighed(block_at):
-        weigh(place, dense, weight, block_at, cap, experts)
-
-    drive(n, weighed, {})
-    for copy in owns:
-        copy.wait()
+    red.flush()
     need("act", "db", "dn")
     tiles = width // TILE
 
@@ -820,11 +818,7 @@
         y = dot(act[e], dn[e, :, s]) + dot(drank_ref[e], db_all[e, slot, :, s])
         part[pl.ds(pl.multiple_of(e * n * cap, 16), n * cap), s] = (y * weight[e]).astype(brain)
 
-    steps = red.steps()
-    drive(
-        experts * tiles, y_tile,
-        {0: steps[0:1], 1: steps[1:2], 2: steps[2:3], 3: steps[3:4], 6: steps[4:5], 8: steps[5:6], 9: steps[6:7]},
-    )
+    drive(experts * tiles, y_tile, {2: steps[4:5], 4: steps[5:6], 5: steps[6:7]})
     seq_ref = dn.at[0]
     loads["seq"] = fetch(seq_hbm, seq_ref, load_sem.at[len(loads) + 4])
     need("resid")
@@ -854,16 +848,21 @@
     drive(
         n, y_block, {2: [functools.partial(bf_g.relay, 0)], 6: [functools.partial(bf_g.relay, 1)]},
     )
+    for i in range(4):
+        redy.give(i)
     for i in range(2, CHUNKS):
         bf_g.relay(i)
-    for i in range(4):
-        redy.give(i)
+    ysteps = redy.steps()
+    for step in ysteps[:4]:
+        step()
     bf_g.pair(bf_g.across)
     mixed_grad(bf_g.across)
-    for i in range(CHUNKS // 2):
-        bf_g.relay_far(i)
+    redy.flush()
+    bf_g.relay_far(0)
     bf_g.pair(bf_g.along)
     mixed_grad(bf_g.along)
+    for i in range(1, CHUNKS // 2):
+        bf_g.relay_far(i)
     bf_g.pair(bf_g.far)
     mixed_grad(bf_g.far)
 
@@ -875,7 +874,6 @@
     swap(1, goa_ref)
 
     need("proj")
-    steps = redy.steps()
     scale = HEAD ** (-0.5)
     block = 256
     for h in range(heads):
@@ -894,15 +892,14 @@
             gk[...] += dot(gs, q, 0, 0)
             gv[...] += dot(probs.astype(brain), do, 0, 0)
 
-        count = (len(steps) + heads - 1) // heads
-        mine_now = steps[h * count : (h + 1) * count]
-        drive(length // block, attend, {i: mine_now[i : i + 1] for i in range(len(mine_now))})
+        drive(length // block, attend, {0: ysteps[4:5], 1: ysteps[5:6], 2: ysteps[6:]} if h == 0 else {})
         gproj[1, :, at] = (gk[...] * scale).astype(brain)
         gproj[2, :, at] = gv[...].astype(brain)
 
     need("a", "b", "w")
     for j in range(3):
         a_ref[16 * j : 16 * j + 16, :] = a_all[j, slot]
+    nsteps = redn.steps()
     for i in range(4):
         p = redn.order[i] // 2
         at = two(p, toks)
@@ -921,7 +918,13 @@
         lax.fori_loop(0, width // wide, normed_grad, 0)
         if i:
             redn.give(i - 1)
+        if i == 2:
+            for step in nsteps[:2]:
+                step()
     redn.give(3)
+    for step in nsteps[2:4]:
+        step()
+    del nsteps[:4]
 
     thin = width // (n * replicas)
 
@@ -932,8 +935,6 @@
                 :, c * thin : (c + 1) * thin
             ].astype(brain)
 
-    nsteps = redn.steps()
-
     def advance():
         if nsteps:
             nsteps.pop(0)()
@@ -942,7 +943,7 @@
         gqb = dot(low_ref[:, 16 * j : 16 * j + 16], gproj[j], 0, 0)
         for d in range(replicas):
             gqb_ref[d, 16 * j : 16 * j + 16, :] = gqb[:, d * piece : (d + 1) * piece].astype(brain)
-    advance()
+    redn.flush()
     got_qb[rep] = gqb_ref[rep]
     swap(0, gqb_ref)
     need("seq")
@@ -1032,7 +1033,7 @@
 
 
 def back(
-    ids, hid, top, gain, gain2, low, lse, orank, dense, drank, resid, seq, proj, mixed, gpart, act, dn, db,
+    ids, hid, top, gain, gain2, low, lse, orank, place, weight, drank, resid, seq, proj, mixed, gpart, act, dn, db,
     w, a, b, wo, pa, pb, pieces, cap, replicas, cid=1,
 ):
     n, toks, width = seq.shape
@@ -1056,12 +1057,11 @@
             h(toks, width), f(toks, width), f(8, 128), h(replicas, 64, thin), h(replicas, 48, piece),
             h(replicas, 16, piece),
         ) + tuple(h(*p.shape) for p in pieces),
-        in_specs=[sm] + [vm] * 9 + [hb] * 18,
+        in_specs=[sm] + [vm] * 10 + [hb] * 18,
         out_specs=[vm] * 10,
         scratch_shapes=[
             fv(toks, width), bv(3, length, span), bv(length, span), bv(4, toks, width), bv(n, toks, width),
-            bv(*act.shape), bv(*dn.shape), bv(*db.shape), bv(experts * rows, width), fv(n * experts, toks),
-            fv(n * experts, toks), fv(experts, rows, 1),
+            bv(*act.shape), bv(*dn.shape), bv(*db.shape), bv(experts * rows, width),
         ]
         + [pltpu.VMEM(v.shape, brain) for v in (w, a, b, wo, pa, pb)]
         + [
@@ -1076,7 +1076,7 @@
         compiler_params=pltpu.CompilerParams(collective_id=cid, has_side_effects=True, vmem_limit_bytes=VMEM_ALL),
         name="back",
     )(
-        ids, hid, top, gain, gain2, low, lse, orank, dense, drank, resid, seq, proj, mixed, gpart, act, dn, db,
+        ids, hid, top, gain, gain2, low, lse, orank, place, weight, drank, resid, seq, proj, mixed, gpart, act, dn, db,
         w, a, b, wo, pa, pb, *pieces,
     )
 
@@ -1217,17 +1217,17 @@
     gain = attention_gain[None]
     gain2 = expert_norm_gain[None]
     hid, cot = hidden[0], output_cotangent[0]
-    low, lse, dense_all, orank, gdr, seq, proj, mixed, resid, x_rows, g_rows, ga = front(
+    low, lse, orank, gdr, place, weight, seq, proj, mixed, resid, x_rows, g_rows, ga = front(
         sequence_adapter, hid, cot, token_experts[0].T, expert_gate_weight[0].T, gain, gain2, query_key_value_weight,
         adapter_attention_input, adapter_attention_output, output_weight, adapter_projection_input,
         adapter_projection_output, down_weight, adapter_down_input, adapter_down_output, n, cap,
     )
     drank, *pieces, gpart, act = moe(
-        sequence_adapter, dense_all, gdr, x_rows, g_rows, ga, gate_up_weight, adapter_hidden_input,
+        sequence_adapter, place, weight, gdr, x_rows, g_rows, ga, gate_up_weight, adapter_hidden_input,
         adapter_hidden_output, adapter_down_input, cap, replicas,
     )
     block_out, grad_hidden, norm, *got = back(
-        sequence_adapter, hid, cot, gain, gain2, low, lse, orank, dense_all, drank, resid, seq, proj, mixed, gpart,
+        sequence_adapter, hid, cot, gain, gain2, low, lse, orank, place, weight, drank, resid, seq, proj, mixed, gpart,
         act, down_weight, adapter_down_output,
         query_key_value_weight, adapter_attention_input, adapter_attention_output, output_weight,
         adapter_projection_input, adapter_projection_output, tuple(pieces), cap, replicas,

time: 259 us -> 252 us (0.973)
  Pallas kernels: 257 us -> 250 us
    pallas_call x1, Pallas kernels: 106 us -> 101 us  [back(): pl.pallas_call(functools.partial(back_kernel, cap, replicas), out_shape=(...]
    pallas_call x1, Pallas kernels: 89.4 us -> 86.5 us  [front(): pl.pallas_call(functools.partial(front_kernel, cap), out_shape=(h(length,...]
where the time goes in v1:
time: 252 us
  Pallas kernels  250 us (99%)
    pallas_call x1, Pallas kernels, back(): pl.pallas_call(functools.partial(back_kernel, cap, replicas), out_shape=(...  101 us
    pallas_call x1, Pallas kernels, front(): pl.pallas_call(functools.partial(front_kernel, cap), out_shape=(h(length,...  86.5 us
    pallas_call x1, Pallas kernels, moe(): pl.pallas_call(functools.partial(moe_kernel, cap, replicas), out_shape=(h...  51.5 us
    pallas_call x1, Pallas kernels, adam(): pl.pallas_call(functools.partial(adam_kernel, n, replicas, groups, spans)...  11 us

profile of v1, /device:TPU:0, one launch (start us, length us, event | category | flops | bytes accessed | tf_op | source)
XLA Modules:
  0.0 251.8 jit_solution(6759959691177805669)
XLA Ops:
  0.7 86.5 %front.1 = (bf16[1024,48]{1,0:T(8,128)(2,1)}, f32[1024,2]{1,0:T(8,128)}, bf16[1024,16]{1,0:T(8,128)(2,1)}, bf16[2,640,16]{2,1,0:T(8,128)(2,1)}, f32[16,128]{1,0:...) custom-call(s32[4]{0:T(128)} %adapter_ref.1, ...), custom_call_target="tpu_custom_call" | custom-call | tf_op jit(solution)/shard_map/front/pallas_call | solution.py:546
  87.2 51.5 %moe.1 = (bf16[2,640,16]{2,1,0:T(8,128)(2,1)}, bf16[4,64,512]{2,1,0:T(8,128)(2,1)}, bf16[4,64,256]{2,1,0:T(8,128)(2,1)}, bf16[4,32,256]{2,1,0:T(8,128)(2,1)}, bf...) custom-call(s32[4]{0:T(128)} %adapter_ref.1, ...), custom_call_target="tpu_custom_call" | custom-call | tf_op jit(solution)/shard_map/moe/pallas_call | solution.py:690
  138.7 101.3 %back.1 = (bf16[128,2048]{1,0:T(8,128)(2,1)}, f32[128,2048]{1,0:T(8,128)}, f32[8,128]{1,0:T(8,128)}, bf16[4,64,64]{2,1,0:T(8,128)(2,1)}, bf16[4,48,64]{2,1,0:T(8...) custom-call(s32[4]{0:T(128)} %adapter_ref.1, ...), custom_call_target="tpu_custom_call" | custom-call | tf_op jit(solution)/shard_map/back/pallas_call | solution.py:1054
  240.6 11.0 %adam.1 = (bf16[128,2048]{1,0:T(8,128)(2,1)}, f32[128,2048]{1,0:T(8,128)}, f32[1]{0:T(128)}, f32[384,64]{1,0:T(8,128)}, f32[384,64]{1,0:T(8,128)}, /*index=5*/f3...) custom-call(s32[4]{0:T(128)} %adapter_ref.1, ...), custom_call_target="tpu_custom_call" | custom-call | tf_op jit(solution)/shard_map/adam/pallas_call | solution.py:1159

commit v2 on v1

--- a/solution.py
+++ b/solution.py
@@ -509,6 +509,9 @@
             return carry
 
         lax.fori_loop(0, 2, one, 0)
+        at = pl.ds(pl.multiple_of(2 * p * cap, 16), 2 * cap)
+        for e in range(experts):
+            save(x_rows.at[e, at], x_hbm.at[e, at])
 
     moe_g.pair(me)
     moe_rows(me)
@@ -522,7 +525,6 @@
     moe_rows(moe_g.along)
     moe_g.pair(moe_g.far)
     moe_rows(moe_g.far)
-    save(x_rows, x_hbm)
     for mover in (seq_g, top_g, red, moe_g):
         mover.drain()
     for copy in saves:
@@ -560,7 +562,7 @@
         + [pltpu.VMEM(v.shape, brain) for v in (w, a, b, wo, pa, pb, dn, da, db)]
         + [
             bv(48, width), bv(3, 48, span), fv(experts * n, toks), fv(n * experts, toks), fv(n, experts * n, toks),
-            pltpu.SemaphoreType.DMA((9,)), pltpu.SemaphoreType.DMA((7,)),
+            pltpu.SemaphoreType.DMA((9,)), pltpu.SemaphoreType.DMA((6 + 4 * experts,)),
         ]
         + gather_scratch(n) + gather_scratch(n) + gather_scratch(n) + scatter_scratch(toks, width)
         + [pltpu.SemaphoreType.DMA((n,)), pltpu.SemaphoreType.DMA((n,))],
@@ -1089,18 +1091,17 @@
     load_sem, save_sem = refs
     me, rep = lax.axis_index("expert"), lax.axis_index("dp")
     common = rep * n + me
-    loads, saves = [], []
-    for a in range(8):
+    loads, saves = {}, []
+    turns = (6, 5, 4, 7, 0, 2, 1, 3)
+    for a in turns:
         size, pieces = spans[a]
         index = common if pieces == n * replicas else rep
         start = index * size // weight[a].shape[1] * weight[a].shape[1]
         view = weight_hbm[a].at[:, pl.ds(pl.multiple_of(start, 128), weight[a].shape[1])]
-        loads.append(
-            [
-                fetch(src, dst, load_sem.at[3 * a + k])
-                for k, (src, dst) in enumerate(((view, weight[a]), (first_hbm[a], first[a]), (second_hbm[a], second[a])))
-            ]
-        )
+        loads[a] = [
+            fetch(src, dst, load_sem.at[3 * a + k])
+            for k, (src, dst) in enumerate(((view, weight[a]), (first_hbm[a], first[a]), (second_hbm[a], second[a])))
+        ]
     saves.append(fetch(out_in, out_hbm, save_sem.at[32]))
     saves.append(fetch(gh_in, gh_hbm, save_sem.at[33]))
     norm_ref[0] = norm_in[0, 0]
@@ -1108,7 +1109,7 @@
     steps = jnp.full((8, 128), step_ref[0].astype(single), single)
     fix_first = (1.0 / (1.0 - jnp.exp(steps * jnp.log(jnp.full((8, 128), beta_one, single)))))[0:1, 0:1]
     fix_second = (1.0 / (1.0 - jnp.exp(steps * jnp.log(jnp.full((8, 128), beta_two, single)))))[0:1, 0:1]
-    for a in (4, 7, 5, 6, 0, 2, 1, 3):
+    for a in turns:
         for copy in loads[a]:
             copy.wait()
         source = got[max(a - 1, 0)]
@@ -1138,11 +1139,14 @@
                 kept[4 * a + 3][at, :] = -learn_rate * (
                     f * fix_first / (jnp.sqrt(s * fix_second) + adam_eps) + weight_decay * w
                 )
+            done = pl.ds(pl.multiple_of(t * ADAPTERS * RANK, ADAPTERS * RANK), ADAPTERS * RANK)
+            for k in range(4 * a, 4 * a + 4):
+                fetch(kept[k].at[done], result[k].at[done], save_sem.at[k])
             return carry
 
         lax.fori_loop(0, groups[a], body, 0)
-        for k in range(4):
-            saves.append(fetch(kept[4 * a + k], result[4 * a + k], save_sem.at[4 * a + k]))
+        for k in range(4 * a, 4 * a + 4):
+            saves.append(pltpu.make_async_copy(kept[k], result[k], save_sem.at[k]))
     for copy in saves:
         copy.wait()
 

time: 252 us -> 250 us (level)
  no operation moved by 1% of the time
where the time goes in v2:
time: 250 us
  Pallas kernels  248 us (99%)
    pallas_call x1, Pallas kernels, back(): pl.pallas_call(functools.partial(back_kernel, cap, replicas), out_shape=(...  101 us
    pallas_call x1, Pallas kernels, front(): pl.pallas_call(functools.partial(front_kernel, cap), out_shape=(h(length,...  85.3 us
    pallas_call x1, Pallas kernels, moe(): pl.pallas_call(functools.partial(moe_kernel, cap, replicas), out_shape=(h...  51.5 us
    pallas_call x1, Pallas kernels, adam(): pl.pallas_call(functools.partial(adam_kernel, n, replicas, groups, spans)...  10.3 us

profile of v2, /device:TPU:0, one launch (start us, length us, event | category | flops | bytes accessed | tf_op | source)
XLA Modules:
  0.0 249.9 jit_solution(898051324540009873)
XLA Ops:
  0.7 85.3 %front.1 = (bf16[1024,48]{1,0:T(8,128)(2,1)}, f32[1024,2]{1,0:T(8,128)}, bf16[1024,16]{1,0:T(8,128)(2,1)}, bf16[2,640,16]{2,1,0:T(8,128)(2,1)}, f32[16,128]{1,0:...) custom-call(s32[4]{0:T(128)} %adapter_ref.1, ...), custom_call_target="tpu_custom_call" | custom-call | tf_op jit(solution)/shard_map/front/pallas_call | solution.py:548
  86.0 51.5 %moe.1 = (bf16[2,640,16]{2,1,0:T(8,128)(2,1)}, bf16[4,64,512]{2,1,0:T(8,128)(2,1)}, bf16[4,64,256]{2,1,0:T(8,128)(2,1)}, bf16[4,32,256]{2,1,0:T(8,128)(2,1)}, bf...) custom-call(s32[4]{0:T(128)} %adapter_ref.1, ...), custom_call_target="tpu_custom_call" | custom-call | tf_op jit(solution)/shard_map/moe/pallas_call | solution.py:692
  137.6 101.3 %back.1 = (bf16[128,2048]{1,0:T(8,128)(2,1)}, f32[128,2048]{1,0:T(8,128)}, f32[8,128]{1,0:T(8,128)}, bf16[4,64,64]{2,1,0:T(8,128)(2,1)}, bf16[4,48,64]{2,1,0:T(8...) custom-call(s32[4]{0:T(128)} %adapter_ref.1, ...), custom_call_target="tpu_custom_call" | custom-call | tf_op jit(solution)/shard_map/back/pallas_call | solution.py:1056
  239.5 10.3 %adam.1 = (bf16[128,2048]{1,0:T(8,128)(2,1)}, f32[128,2048]{1,0:T(8,128)}, f32[1]{0:T(128)}, f32[384,64]{1,0:T(8,128)}, f32[384,64]{1,0:T(8,128)}, /*index=5*/f3...) custom-call(s32[4]{0:T(128)} %adapter_ref.1, ...), custom_call_target="tpu_custom_call" | custom-call | tf_op jit(solution)/shard_map/adam/pallas_call | solution.py:1163

commit v3 on v2

--- a/solution.py
+++ b/solution.py
@@ -649,13 +649,15 @@
         g_copy(e).wait()
         deal(gdnb_ref, e * 16, dot((drank_ref[e].astype(single) * weight[e]).astype(brain), g_rows[e], 0, 0))
 
+        wide = min(2 * TILE, width)
+
         def slots(d, c):
-            at = cols(d)
+            at = pl.ds(pl.multiple_of(d * wide, wide), wide)
             s = dot(gg[...], gu[e, 0, at, :], 1, 1) + dot(uu[...], gu[e, 1, at, :], 1, 1)
             s_rows[pl.ds(pl.multiple_of(e * rows, 16), rows), at] = (s + dot(girank[...], ha_ref[e, :, at])).astype(brain)
             return c
 
-        lax.fori_loop(0, width // TILE, slots, 0)
+        lax.fori_loop(0, width // wide, slots, 0)
         return carry
 
     lax.fori_loop(0, experts, expert, 0)

time: 250 us -> 248 us (level)
  no operation moved by 1% of the time
where the time goes in v3:
time: 248 us
  Pallas kernels  246 us (99%)
    pallas_call x1, Pallas kernels, back(): pl.pallas_call(functools.partial(back_kernel, cap, replicas), out_shape=(...  101 us
    pallas_call x1, Pallas kernels, front(): pl.pallas_call(functools.partial(front_kernel, cap), out_shape=(h(length,...  85.4 us
    pallas_call x1, Pallas kernels, moe(): pl.pallas_call(functools.partial(moe_kernel, cap, replicas), out_shape=(h...  49.9 us
    pallas_call x1, Pallas kernels, adam(): pl.pallas_call(functools.partial(adam_kernel, n, replicas, groups, spans)...  10.3 us

profile of v3, /device:TPU:0, one launch (start us, length us, event | category | flops | bytes accessed | tf_op | source)
XLA Modules:
  0.0 248.0 jit_solution(12148640993908633238)
XLA Ops:
  0.7 85.4 %front.1 = (bf16[1024,48]{1,0:T(8,128)(2,1)}, f32[1024,2]{1,0:T(8,128)}, bf16[1024,16]{1,0:T(8,128)(2,1)}, bf16[2,640,16]{2,1,0:T(8,128)(2,1)}, f32[16,128]{1,0:...) custom-call(s32[4]{0:T(128)} %adapter_ref.1, ...), custom_call_target="tpu_custom_call" | custom-call | tf_op jit(solution)/shard_map/front/pallas_call | solution.py:548
  86.0 49.9 %moe.1 = (bf16[2,640,16]{2,1,0:T(8,128)(2,1)}, bf16[4,64,512]{2,1,0:T(8,128)(2,1)}, bf16[4,64,256]{2,1,0:T(8,128)(2,1)}, bf16[4,32,256]{2,1,0:T(8,128)(2,1)}, bf...) custom-call(s32[4]{0:T(128)} %adapter_ref.1, ...), custom_call_target="tpu_custom_call" | custom-call | tf_op jit(solution)/shard_map/moe/pallas_call | solution.py:694
  135.9 101.0 %back.1 = (bf16[128,2048]{1,0:T(8,128)(2,1)}, f32[128,2048]{1,0:T(8,128)}, f32[8,128]{1,0:T(8,128)}, bf16[4,64,64]{2,1,0:T(8,128)(2,1)}, bf16[4,48,64]{2,1,0:T(8...) custom-call(s32[4]{0:T(128)} %adapter_ref.1, ...), custom_call_target="tpu_custom_call" | custom-call | tf_op jit(solution)/shard_map/back/pallas_call | solution.py:1058
  237.6 10.3 %adam.1 = (bf16[128,2048]{1,0:T(8,128)(2,1)}, f32[128,2048]{1,0:T(8,128)}, f32[1]{0:T(128)}, f32[384,64]{1,0:T(8,128)}, f32[384,64]{1,0:T(8,128)}, /*index=5*/f3...) custom-call(s32[4]{0:T(128)} %adapter_ref.1, ...), custom_call_target="tpu_custom_call" | custom-call | tf_op jit(solution)/shard_map/adam/pallas_call | solution.py:1165
